TPU v7x, 32 devices: a whole 2x2x4 slice. The times are simulated.
32 devices in a mesh: dp: 4 (over y, x), sub: 8 (over z, core).
Axes of the slice: x: 2, y: 2, z: 4, core: 2. Of those that a mesh axis runs over, the one named last changes fastest.
Arguments:
- embeddings: bfloat16 [12288, 1024], P('dp'), may hold values from -4096 to 4096
- assignment: int32 [12288], P('dp'), may hold values from 0 to 4095
- centroids: bfloat16 [4096, 1024], P('sub'), may hold values from -1 to 1
- codebooks: float32 [64, 16, 256], P('sub'), may hold values from -2 to 2
Outputs:
- new_centroids: float32 [4096, 1024], P('sub')
- new_codebooks: float32 [64, 16, 256], P('sub')
All inputs are finite; a program needn't handle non-finite values.
Results may differ from a plain program's by a relative error of at most 0.0004.
The roundings to bfloat16 on the way count: a program that leaves them out, or rounds other values in their place, can miss the bound.
Values may be sent and summed in bfloat16 or wider, within the bound.
No kernel may reach another device: no remote copies, remote signals or barrier semaphores. Data moves between devices by JAX's collectives and lax.ppermute only.
A program may use at most 128 MiB of HBM per device.

v0:
```python
import functools
import math

import jax
import jax.numpy as jnp
from jax import lax
from jax.experimental import pallas as pl
from jax.experimental.pallas import tpu as pltpu
from jax.sharding import PartitionSpec as P


F32 = jnp.float32
BF16 = jnp.bfloat16
VMEM = pltpu.VMEM
SMEM = pltpu.SMEM
NT = (((1,), (1,)), ((), ()))


def swap(value, axis, size, hop):
    return lax.ppermute(value, axis, [(i, i ^ hop) for i in range(size)])


def block_of(extent, want):
    return want if extent % want == 0 else extent


def params(limit=32 << 20):
    return pltpu.CompilerParams(vmem_limit_bytes=limit)


def encode(value, extra, code_ref):
    rows, feat = value.shape
    lane = lax.broadcasted_iota(jnp.int32, (rows, 128), 1)
    tail = jnp.zeros((rows, 128), F32)
    pieces = [value[:, at : at + 128] for at in range(0, feat, 128)]
    if extra is not None:
        pieces.append(extra)
    for at, piece in enumerate(pieces):
        peak = jnp.maximum(jnp.max(jnp.abs(piece), axis=1, keepdims=True), 1e-30)
        exponent = jnp.floor(jnp.log2(peak) * 16.0) + 1.5
        code = jnp.round(piece * (32000.0 * jnp.exp2(exponent * (-1.0 / 16.0))))
        tail = jnp.where(lane == at, exponent - 0.5, tail)
        if at * 128 < feat:
            code_ref[:, at * 128 : (at + 1) * 128] = code.astype(jnp.int32).astype(jnp.int16)
        else:
            tail = jnp.where(lane == 127, code, tail)
    code_ref[:, feat:] = tail.astype(jnp.int32).astype(jnp.int16)


def decode(code_ref):
    feat = code_ref.shape[1] - 128
    tail = code_ref[:, feat:].astype(jnp.int32).astype(F32)
    scale = (1.0 / 32000.0) / jnp.exp2((tail + 0.5) * (-1.0 / 16.0))
    pieces = [
        code_ref[:, at : at + 128].astype(jnp.int32).astype(F32) * scale[:, at // 128 : at // 128 + 1]
        for at in range(0, feat, 128)
    ]
    return pieces, tail[:, 127:128] * scale[:, feat // 128 : feat // 128 + 1]


def table_kernel(pos_ref, cent_ref, *refs, width):
    outs, flip_ref = refs[:-1], refs[-1]
    flip_ref[...] = cent_ref[...].T
    for hop, out_ref in enumerate(outs):
        start = pl.multiple_of((pos_ref[0] ^ hop) * width, width)
        out_ref[...] = flip_ref[pl.ds(start, width), :]


def table_parts(position, centroids, peers):
    local_k, feat = centroids.shape
    width = feat // peers
    return pl.pallas_call(
        functools.partial(table_kernel, width=width),
        out_shape=[jax.ShapeDtypeStruct((width, local_k), BF16)] * peers,
        in_specs=[pl.BlockSpec(memory_space=SMEM), pl.BlockSpec(memory_space=VMEM)],
        out_specs=[pl.BlockSpec(memory_space=VMEM)] * peers,
        scratch_shapes=[VMEM((feat, local_k), BF16)],
        compiler_params=params(),
        name="table_parts",
    )(position, centroids)


def logits_kernel(cent_ref, rows_ref, logits_ref, stats_ref, half_ref):
    @pl.when(pl.program_id(0) == 0)
    def _():
        wide = cent_ref[...].astype(F32)
        half_ref[...] = jnp.broadcast_to(
            0.5 * jnp.sum(wide * wide, axis=1, keepdims=True), half_ref.shape
        )

    logits = (
        lax.dot_general(cent_ref[...], rows_ref[...], NT, preferred_element_type=F32)
        - half_ref[:, 0:1]
    )
    logits_ref[...] = logits
    peak = jnp.max(logits, axis=0, keepdims=True)
    stats_ref[0:1, :] = peak
    stats_ref[1:2, :] = jnp.sum(jnp.exp(logits - peak), axis=0, keepdims=True)


def local_logits(centroids, embeddings):
    local_k, feat = centroids.shape
    rows = embeddings.shape[0]
    block = block_of(rows, 1024)
    return pl.pallas_call(
        logits_kernel,
        grid=(rows // block,),
        out_shape=[
            jax.ShapeDtypeStruct((local_k, rows), F32),
            jax.ShapeDtypeStruct((2, rows), F32),
        ],
        in_specs=[
            pl.BlockSpec((local_k, feat), lambda i: (0, 0)),
            pl.BlockSpec((block, feat), lambda i: (i, 0)),
        ],
        out_specs=[
            pl.BlockSpec((local_k, block), lambda i: (0, i)),
            pl.BlockSpec((2, block), lambda i: (0, i)),
        ],
        scratch_shapes=[VMEM((local_k, 128), F32)],
        compiler_params=params(),
        cost_estimate=pl.CostEstimate(
            flops=2 * local_k * rows * feat,
            transcendentals=local_k * rows,
            bytes_accessed=rows * feat * 2 + local_k * rows * 4,
        ),
        name="local_logits",
    )(centroids, embeddings)


def merge(former, latter):
    peak = jnp.maximum(former[0:1], latter[0:1])
    total = former[1:2] * jnp.exp(former[0:1] - peak) + latter[1:2] * jnp.exp(latter[0:1] - peak)
    return jnp.concatenate([peak, total], axis=0)


def sums_kernel(pos_ref, logits_ref, stats_ref, rows_ref, *refs, peers):
    own_ref, own_count_ref = refs[:2]
    outs, (acc_ref, count_ref) = refs[2 : peers + 1], refs[peers + 1 :]
    step = pl.program_id(0)
    probability = jnp.exp(logits_ref[...] - stats_ref[0:1, :]) * (1.0 / stats_ref[1:2, :])
    partial = probability[:, 0:128]
    for lane in range(128, probability.shape[1], 128):
        partial = partial + probability[:, lane : lane + 128]
    sums = jnp.dot(probability.astype(BF16), rows_ref[...], preferred_element_type=F32)

    @pl.when(step == 0)
    def _():
        acc_ref[...] = sums
        count_ref[...] = partial

    @pl.when(step > 0)
    def _():
        acc_ref[...] += sums
        count_ref[...] += partial

    @pl.when(step == pl.num_programs(0) - 1)
    def _():
        part = own_ref.shape[0]
        for hop in range(peers):
            start = pl.multiple_of((pos_ref[0] ^ hop) * part, part)
            count = jnp.sum(count_ref[pl.ds(start, part), :], axis=1, keepdims=True)
            if hop == 0:
                own_ref[...] = acc_ref[pl.ds(start, part), :]
                own_count_ref[...] = jnp.broadcast_to(count, own_count_ref.shape)
            else:
                encode(acc_ref[pl.ds(start, part), :], count, outs[hop - 1])


def local_sums(position, logits, stats, embeddings, peers):
    local_k, rows = logits.shape
    feat = embeddings.shape[1]
    block = block_of(rows, 1024)
    part = local_k // peers
    whole = lambda shape: pl.BlockSpec(shape, lambda i: (0, 0))
    return pl.pallas_call(
        functools.partial(sums_kernel, peers=peers),
        grid=(rows // block,),
        out_shape=[jax.ShapeDtypeStruct((part, feat), F32), jax.ShapeDtypeStruct((part, 128), F32)]
        + [jax.ShapeDtypeStruct((part, feat + 128), jnp.int16)] * (peers - 1),
        in_specs=[
            pl.BlockSpec(memory_space=SMEM),
            pl.BlockSpec((local_k, block), lambda i: (0, i)),
            pl.BlockSpec((2, block), lambda i: (0, i)),
            pl.BlockSpec((block, feat), lambda i: (i, 0)),
        ],
        out_specs=[whole((part, feat)), whole((part, 128))]
        + [whole((part, feat + 128))] * (peers - 1),
        scratch_shapes=[VMEM((local_k, feat), F32), VMEM((local_k, 128), F32)],
        compiler_params=params(),
        cost_estimate=pl.CostEstimate(
            flops=2 * local_k * rows * feat,
            transcendentals=local_k * rows,
            bytes_accessed=rows * feat * 2 + local_k * rows * 4,
        ),
        name="local_sums",
    )(position, logits, stats, embeddings)


def update_kernel(pos_ref, cent_ref, own_ref, own_count_ref, *refs):
    codes, out_ref = refs[:-1], refs[-1]
    part, feat = own_ref.shape
    count = own_count_ref[:, 0:1]
    total = [own_ref[:, lane : lane + 128] for lane in range(0, feat, 128)]
    for code in codes:
        pieces, more = decode(code)
        count = count + more
        total = [former + latter for former, latter in zip(total, pieces)]
    start = pl.multiple_of(pos_ref[0] * part, part)
    cent = cent_ref[pl.ds(start, part), :].astype(F32)
    encode((jnp.concatenate(total, axis=1) + cent) / (count + 1.0), None, out_ref)


def update_part(position, centroids, own, own_count, codes):
    return pl.pallas_call(
        update_kernel,
        out_shape=jax.ShapeDtypeStruct(codes[0].shape, jnp.int16),
        in_specs=[pl.BlockSpec(memory_space=SMEM)] + [pl.BlockSpec(memory_space=VMEM)] * (3 + len(codes)),
        out_specs=pl.BlockSpec(memory_space=VMEM),
        compiler_params=params(16 << 20),
        name="update_part",
    )(position, centroids, own, own_count, *codes)


def join_kernel(pos_ref, *refs):
    codes, out_ref = refs[:-1], refs[-1]
    size = codes[0].shape[0]
    for hop, code in enumerate(codes):
        start = pl.multiple_of((pos_ref[0] ^ hop) * size, size)
        for at, piece in enumerate(decode(code)[0]):
            out_ref[pl.ds(start, size), at * 128 : (at + 1) * 128] = piece


def join_parts(position, codes):
    size, feat = codes[0].shape
    return pl.pallas_call(
        join_kernel,
        out_shape=jax.ShapeDtypeStruct((size * len(codes), feat - 128), F32),
        in_specs=[pl.BlockSpec(memory_space=SMEM)] + [pl.BlockSpec(memory_space=VMEM)] * len(codes),
        out_specs=pl.BlockSpec(memory_space=VMEM),
        compiler_params=params(16 << 20),
        name="join_parts",
    )(position, *codes)


def three_terms(value):
    first = value.astype(BF16)
    rest = value - first.astype(F32)
    second = rest.astype(BF16)
    third = (rest - second.astype(F32)).astype(BF16)
    return first, second, third


def codes_kernel(pick_ref, feats_ref, code_ref, *refs, peers, half):
    former = refs[peers : peers + 1]
    refs = refs[:peers] + refs[-5:]
    tables, (out_ref, table_ref, weight_ref, data_ref, acc_ref) = refs[:peers], refs[peers:]
    step = pl.program_id(0)
    groups, sub_dim, words = code_ref.shape
    width, local_k = tables[0].shape
    first_feat = half * width
    block = feats_ref.shape[0]
    head = 3 * sub_dim

    @pl.when(step == 0)
    def _():
        for hop in range(peers):
            table_ref[hop * width : (hop + 1) * width, :] = tables[hop][...]
        scale = 1.0 / math.log(2.0)
        lane_row = lax.broadcasted_iota(jnp.int32, (sub_dim, words), 0)
        for group in range(groups):
            code = code_ref[group]
            first, second, third = three_terms(code * scale)
            half = -0.5 * scale * jnp.sum(code * code, axis=0, keepdims=True)
            bias = [jnp.broadcast_to(t.astype(F32), (sub_dim, words)) for t in three_terms(half)]
            bias = jnp.where(
                lane_row == 0, bias[0], jnp.where(lane_row == 1, bias[1], jnp.where(lane_row == 2, bias[2], 0.0))
            )
            first, second, third = (t.astype(F32) for t in (first, second, third))
            stacked = jnp.concatenate([first, first, bias, second, second, third, third], axis=0)
            weight_ref[group * words : (group + 1) * words, :] = stacked.T.astype(BF16)
        acc_ref[...] = jnp.zeros_like(acc_ref)
        for group in range(groups):
            data_ref[group, 2 * sub_dim : 3 * sub_dim, :] = jnp.ones((sub_dim, block), BF16)

    source, entry = pick_ref[0:1, :], pick_ref[1:2, :]
    hot = (lax.broadcasted_iota(jnp.int32, (local_k, block), 0) == entry).astype(F32).astype(BF16)
    slabs = jnp.dot(table_ref[...], hot, preferred_element_type=F32)
    base = slabs[0:width]
    for hop in range(1, peers):
        base = jnp.where(source == hop, slabs[hop * width : (hop + 1) * width], base)
    minus = (-base).astype(BF16)
    own = feats_ref[...].astype(F32).T.astype(BF16)[first_feat : first_feat + width]
    for group in range(groups):
        span = slice(group * sub_dim, (group + 1) * sub_dim)
        for at in (0, 3, 5):
            data_ref[group, at * sub_dim : (at + 1) * sub_dim, :] = own[span]
            data_ref[group, (at + 1) * sub_dim : (at + 2) * sub_dim, :] = minus[span]
    for group in range(groups):
        logits = jnp.dot(
            weight_ref[group * words : (group + 1) * words, :], data_ref[group], preferred_element_type=F32
        )
        expo = jnp.exp2(logits - jnp.max(logits, axis=0, keepdims=True))
        weights = expo * (1.0 / jnp.sum(expo, axis=0, keepdims=True))
        high = weights.astype(BF16)
        low = (weights - high.astype(F32)).astype(BF16)
        left = data_ref[group, 0:head, :]
        acc_ref[group] += lax.dot_general(high, left, NT, preferred_element_type=F32) + lax.dot_general(
            low, left, NT, preferred_element_type=F32
        )

    @pl.when(step == pl.num_programs(0) - 1)
    def _():
        if half:
            out_ref[0 : former[0].shape[0], :] = former[0][...]
        first_row, first_count = half * groups * sub_dim, out_ref.shape[0] - (half + 1) * groups
        if half:
            out_ref[first_count + groups :, :] = former[0][half * groups * sub_dim :, :]
        for group in range(groups):
            found = acc_ref[group].T
            row = first_row + group * sub_dim
            out_ref[row : row + sub_dim, :] = found[0:sub_dim] + found[sub_dim : 2 * sub_dim]
            out_ref[first_count + group : first_count + group + 1, :] = found[2 * sub_dim : 2 * sub_dim + 1]


def local_codes(pick, features, codebooks, tables, half, halves, former=(), after=()):
    peers = len(tables)
    rows, feats = features.shape
    local_k = tables[0].shape[1]
    groups, sub_dim, words = codebooks.shape
    groups, width = groups // halves, feats // halves
    block = block_of(rows, 1536)
    depth = 7 * sub_dim
    fixed = lambda shape: pl.BlockSpec(shape, lambda i: (0,) * len(shape))
    return pl.pallas_call(
        functools.partial(codes_kernel, peers=peers, half=half),
        grid=(rows // block,),
        out_shape=jax.ShapeDtypeStruct(((half + 1) * groups * (sub_dim + 1), words), F32),
        in_specs=[
            pl.BlockSpec((2, block), lambda i: (0, i)),
            pl.BlockSpec((block, feats), lambda i: (i, 0)),
            pl.BlockSpec((groups, sub_dim, words), lambda i: (half, 0, 0)),
        ]
        + [pl.BlockSpec((width, local_k), lambda i: (half, 0))] * peers
        + [fixed(each.shape) for each in former]
        + [pl.BlockSpec(memory_space=pl.ANY)] * len(after),
        out_specs=fixed(((half + 1) * groups * (sub_dim + 1), words)),
        scratch_shapes=[
            VMEM((peers * width, local_k), BF16),
            VMEM((groups * words, depth), BF16),
            VMEM((groups, depth, block), BF16),
            VMEM((groups, words, 3 * sub_dim), F32),
        ],
        compiler_params=params(),
        cost_estimate=pl.CostEstimate(
            flops=2 * rows * (peers * width * local_k + groups * words * 256 * 3),
            transcendentals=rows * groups * words,
            bytes_accessed=rows * width * 2 + peers * width * local_k * 2,
        ),
    )(pick, features, codebooks, *tables, *former, *after)


def after(value, *others):
    return lax.optimization_barrier((value, *others))[0]


def shards(embeddings, assignment, centroids, codebooks):
    n_sub, n_dp = lax.axis_size("sub"), lax.axis_size("dp")
    sub_at, dp_at = lax.axis_index("sub"), lax.axis_index("dp")
    sub_pos, dp_pos = sub_at[None].astype(jnp.int32), dp_at[None].astype(jnp.int32)
    local_k = centroids.shape[0]
    width = embeddings.shape[1] // n_sub
    groups, sub_dim, words = codebooks.shape
    hops = range(1, n_dp)

    parts = table_parts(sub_pos, centroids, n_sub)
    tables = [parts[0]] + [None] * (n_sub - 1)

    def send_table(hop, *others):
        tables[hop] = swap(after(parts[hop], *others), "sub", n_sub, hop)

    for hop in EARLY:
        send_table(hop)
    logits, stats = local_logits(centroids, embeddings)
    hop = 1
    while hop < n_sub:
        other = swap(stats, "sub", n_sub, hop)
        stats = merge(stats, other)
        hop *= 2
    for hop in range(n_sub - 1, 0, -1):
        if tables[hop] is None:
            send_table(hop, stats)

    found = local_sums(dp_pos, logits, stats, embeddings, n_dp)
    own, own_count, sums = found[0], found[1], list(found[2:])
    for hop in hops:
        sums[hop - 1] = swap(sums[hop - 1], "dp", n_dp, hop)
    code = update_part(dp_pos, centroids, own, own_count, sums)
    updated = [code]
    for hop in hops:
        updated.append(swap(code, "dp", n_dp, hop))
    new_centroids = join_parts(dp_pos, updated)

    pick = jnp.stack([(assignment // local_k) ^ sub_at, assignment % local_k]).astype(jnp.int32)
    features = lax.dynamic_slice_in_dim(embeddings, sub_at * width, width, 1)
    found = local_codes(pick, features, codebooks, tables, 0, 2)
    found = local_codes(pick, features, codebooks, tables, 1, 2, (found,), (code,))
    pieces = [found]
    for hop in hops:
        pieces.append(swap(found, "dp", n_dp, hop))
    while len(pieces) > 1:
        pieces = [pieces[i] + pieces[i + 1] for i in range(0, len(pieces), 2)]
    total, each = pieces[0], groups // 2
    code_sums = total[: groups * sub_dim].reshape(groups, sub_dim, words)
    code_counts = jnp.concatenate([total[groups * sub_dim + each :], total[groups * sub_dim : groups * sub_dim + each]])
    new_codebooks = (code_sums + codebooks) / (code_counts[:, None, :] + 1.0)
    return (new_centroids, new_codebooks)


EARLY = (6, 7, 2, 3)


def solution(mesh):
    placed = (P("dp", None), P("dp"), P("sub", None), P("sub", None, None))
    return jax.shard_map(
        shards,
        mesh=mesh,
        in_specs=placed,
        out_specs=(P("sub", None), P("sub", None, None)),
        check_vma=False,
    )
```

profile of v0, /device:TPU:0, one launch (start us, length us, event | category | flops | bytes accessed | tf_op | source)
XLA Modules:
  0.0 101.5 jit_solution(6668162874714266162)
XLA Ops:
  0.6 0.0 copy-start
  0.6 2.8 %copy-done = bf16[3072,1024]{1,0:T(8,128)(2,1)S(1)} copy-done((bf16[3072,1024]{1,0:T(8,128)(2,1)S(1)}, bf16[3072,1024]{1,0:T(8,128)(2,1)}, u32[]{:S(2)}) %copy-start) | copy-done | bytes 6291480
  3.4 0.0 copy-start.4
  3.4 1.2 %copy-done.4 = bf16[512,1024]{1,0:T(8,128)(2,1)S(1)} copy-done((bf16[512,1024]{1,0:T(8,128)(2,1)S(1)}, bf16[512,1024]{1,0:T(8,128)(2,1)}, u32[]{:S(2)}) %copy-start.4) | copy-done | bytes 1048600
  4.6 0.0 copy-start.5
  4.6 0.0 copy-start.7
  4.6 5.6 %local_logits.1 = (f32[512,3072]{1,0:T(8,128)S(1)}, f32[2,3072]{1,0:T(2,128)S(1)}) custom-call(bf16[512,1024]{1,0:T(8,128)(2,1)S(1)} %copy-done.4, bf16[3072,1024]{1,0:T(8,128)(2,1)S(1)} %copy-done), custom_call_target="tpu_custom_call" | custom-call | flops 3221225472 | bytes 12582912 | tf_op jit(solution)/shard_map/local_logits/pallas_call | solution.py:105
  10.2 0.0 copy-start.2
  10.3 2.6 %copy-done.2 = f32[512,3072]{1,0:T(8,128)} copy-done((f32[512,3072]{1,0:T(8,128)}, f32[512,3072]{1,0:T(8,128)S(1)}, u32[]{:S(2)}) %copy-start.2) | copy-done | bytes 6291480
  12.9 0.5 collective-permute-start
  13.4 0.0 copy-done.5
  13.4 0.4 table_parts.1
  13.8 2.6 %collective-permute-start.10 = (bf16[128,512]{1,0:T(8,128)(2,1)S(1)}, bf16[128,512]{1,0:T(8,128)(2,1)S(1)}, u32[]{:S(2)}, u32[]{:S(2)}) collective-permute-start(bf16[128,512]{1,0:T(8,128)(2,1)S(1)} %get-tuple-element.30), channel_id=1, source_target_pairs={{0,2},{1,3},{2,0},{3,1},{4,6},{5,7},{6,4},{7,5},{8,10},{9,11},{10,... | collective-permute-start | bytes 393224 | tf_op jit(solution)/shard_map/ppermute | solution.py:20
  16.4 0.2 collective-permute-start.11
  16.6 3.7 %collective-permute-start.14 = (bf16[128,512]{1,0:T(8,128)(2,1)S(1)}, bf16[128,512]{1,0:T(8,128)(2,1)S(1)}, u32[]{:S(2)}, u32[]{:S(2)}) collective-permute-start(bf16[128,512]{1,0:T(8,128)(2,1)S(1)} %get-tuple-element.36), channel_id=1, source_target_pairs={{0,6},{1,7},{2,4},{3,5},{4,2},{5,3},{6,0},{7,1},{8,14},{9,15},{10,... | collective-permute-start | bytes 393224 | tf_op jit(solution)/shard_map/ppermute | solution.py:20
  20.3 0.0 collective-permute-start.15
  20.3 1.2 %constant_dynamic-slice_fusion.feats_ref = bf16[3072,128]{1,0:T(8,128)(2,1)S(1)} fusion(bf16[3072,1024]{1,0:T(8,128)(2,1)} %rows_ref.3, s32[]{:T(128)S(6)} %select_n.17), kind=kLoop, calls=%fused_computation.25 | loop fusion | bytes 1572868 | tf_op jit(solution)/shard_map/dynamic_slice | solution.py:405
  21.5 0.0 collective-permute-done
  21.5 0.1 fusion.3
  21.6 0.1 collective-permute-start.1
  21.7 0.0 copy-done.7
  21.7 7.1 %collective-permute-done.1 = f32[2,3072]{1,0:T(2,128)S(1)} collective-permute-done((f32[2,3072]{1,0:T(2,128)S(1)}, f32[2,3072]{1,0:T(2,128)S(1)}, u32[]{:S(2)}, u32[]{:S(2)}) %collective-permute-start.1) | collective-permute-done | bytes 24608 | tf_op jit(solution)/shard_map/ppermute | solution.py:20
  28.9 3.5 %collective-permute-start.2 = (f32[2,3072]{1,0:T(2,128)S(1)}, f32[2,3072]{1,0:T(2,128)S(1)}, u32[]{:S(2)}, u32[]{:S(2)}) collective-permute-start(f32[2,3072]{1,0:T(2,128)S(1)} %pad_maximum_fusion.1), channel_id=1, source_target_pairs={{0,4},{1,5},{2,6},{3,7},{4,0},{5,1},{6,2},{7,3},{8,12},{9,13},{10,... | collective-permute-start | bytes 73736 | tf_op jit(solution)/shard_map/ppermute | solution.py:20
  32.5 1.8 %collective-permute-done.2 = f32[2,3072]{1,0:T(2,128)S(1)} collective-permute-done((f32[2,3072]{1,0:T(2,128)S(1)}, f32[2,3072]{1,0:T(2,128)S(1)}, u32[]{:S(2)}, u32[]{:S(2)}) %collective-permute-start.2) | collective-permute-done | bytes 24608 | tf_op jit(solution)/shard_map/ppermute | solution.py:20
  34.4 0.1 collective-permute-start.9
  34.4 0.0 collective-permute-done.10.refs_2_
  34.4 3.0 %collective-permute-start.12 = (bf16[128,512]{1,0:T(8,128)(2,1)S(1)}, bf16[128,512]{1,0:T(8,128)(2,1)S(1)}, u32[]{:S(2)}, u32[]{:S(2)}) collective-permute-start(bf16[128,512]{1,0:T(8,128)(2,1)S(1)} %get-tuple-element.33), channel_id=1, source_target_pairs={{0,4},{1,5},{2,6},{3,7},{4,0},{5,1},{6,2},{7,3},{8,12},{9,13},{10,... | collective-permute-start | bytes 393224 | tf_op jit(solution)/shard_map/ppermute | solution.py:20
  37.4 0.0 collective-permute-done.11.refs_3_
  37.5 0.1 collective-permute-start.13
  37.6 0.0 copy-start.1
  37.6 2.8 %copy-done.1 = bf16[3072,1024]{1,0:T(8,128)(2,1)S(1)} copy-done((bf16[3072,1024]{1,0:T(8,128)(2,1)S(1)}, bf16[3072,1024]{1,0:T(8,128)(2,1)}, u32[]{:S(2)}) %copy-start.1) | copy-done | bytes 6291480
  40.3 0.0 copy-start.3
  40.3 2.8 %copy-done.3 = f32[512,3072]{1,0:T(8,128)S(1)} copy-done((f32[512,3072]{1,0:T(8,128)S(1)}, f32[512,3072]{1,0:T(8,128)}, u32[]{:S(2)}) %copy-start.3) | copy-done | bytes 6291480
  43.1 0.0 copy-start.6
  43.1 5.8 %local_sums.1 = (f32[128,1024]{1,0:T(8,128)S(1)}, f32[128,128]{1,0:T(8,128)S(1)}, s16[128,1152]{1,0:T(8,128)(2,1)S(1)}, s16[128,1152]{1,0:T(8,128)(2,1)S(1)}, s16[128,1152]{1,0:T(8,128)(2,1)S(1)}) custom-call(s32[1]{0:T(128)} %bitcast.pos_ref, f32[512,3072]{1,0:T(8,128)S(1)} %copy-done.3, f32[2,3072]{1,0:T(2,128)S(1)} %pad_maximum_fusion.2.stats_ref, ...), custom_call_target="tpu_custom_call" | custom-call | flops 3221225472 | bytes 12582912 | tf_op jit(solution)/shard_map/local_sums/pallas_call | solution.py:176
  48.9 0.0 collective-permute-done.14.refs_6_
  48.9 1.6 %collective-permute-start.3 = (s16[128,1152]{1,0:T(8,128)(2,1)S(1)}, s16[128,1152]{1,0:T(8,128)(2,1)S(1)}, u32[]{:S(2)}, u32[]{:S(2)}) collective-permute-start(s16[128,1152]{1,0:T(8,128)(2,1)S(1)} %get-tuple-element.24), channel_id=1, source_target_pairs={{0,8},{8,0},{16,24},{24,16},{1,9},{9,1},{17,25},{25,17},{2,10},{10... | collective-permute-start | bytes 884744 | tf_op jit(solution)/shard_map/ppermute | solution.py:20
  50.5 0.0 collective-permute-done.15.refs_7_
  50.5 1.5 %collective-permute-start.4 = (s16[128,1152]{1,0:T(8,128)(2,1)S(1)}, s16[128,1152]{1,0:T(8,128)(2,1)S(1)}, u32[]{:S(2)}, u32[]{:S(2)}) collective-permute-start(s16[128,1152]{1,0:T(8,128)(2,1)S(1)} %get-tuple-element.25), channel_id=1, source_target_pairs={{0,16},{8,24},{16,0},{24,8},{1,17},{9,25},{17,1},{25,9},{2,18},{10... | collective-permute-start | bytes 884744 | tf_op jit(solution)/shard_map/ppermute | solution.py:20
  52.0 0.0 collective-permute-done.9.refs_1_
  52.0 0.5 collective-permute-start.5
  52.5 0.0 collective-permute-done.12.refs_4_
  52.5 0.0 collective-permute-done.13.refs_5_
  52.5 0.0 copy-done.6
  52.5 10.3 %shard_map.59.refs_8_ = f32[68,256]{1,0:T(8,128)S(1)} custom-call(s32[2,3072]{1,0:T(2,128)S(1)} %pad_add_fusion.pick_ref, bf16[3072,128]{1,0:T(8,128)(2,1)S(1)} %constant_dynamic-slice_fusion.feats_ref, f32[8,16,256]{2,1,0:T(8,128)S(1)} %copy-done.6, bf16[128,512]{1,0:T(8,128)(2,1)S(1)} %get-tuple-element.27.refs_0_, ...), custom_call_target="tpu_custom_call" | custom-call | flops 6442450944 | bytes 917504 | tf_op jit(solution)/shard_map/pallas_call | solution.py:335
  62.8 0.0 collective-permute-done.3.refs_0_
  62.9 2.7 %collective-permute-done.4.refs_1_ = s16[128,1152]{1,0:T(8,128)(2,1)S(1)} collective-permute-done((s16[128,1152]{1,0:T(8,128)(2,1)S(1)}, s16[128,1152]{1,0:T(8,128)(2,1)S(1)}, u32[]{:S(2)}, u32[]{:S(2)}) %collective-permute-start.4) | collective-permute-done | bytes 294944 | tf_op jit(solution)/shard_map/ppermute | solution.py:20
  65.6 0.0 collective-permute-done.5.refs_2_
  65.6 1.2 %update_part.1.refs_0_.refs_9_ = s16[128,1152]{1,0:T(8,128)(2,1)S(1)} custom-call(s32[1]{0:T(128)} %bitcast.pos_ref, bf16[512,1024]{1,0:T(8,128)(2,1)S(1)} %copy-done.5, f32[128,1024]{1,0:T(8,128)S(1)} %get-tuple-element.22.own_ref, f32[128,128]{1,0:T(8,128)S(1)} %get-tuple-element.23.own_count_ref, s16[128,1152]{1,0:T(8,128)(2,1)S(1)} %collective-permute-done.3.refs_0_, ...), custom_call_target="tpu_custom_call" | custom-call | tf_op jit(solution)/shard_map/update_part/pallas_call | solution.py:215
  66.8 10.2 %shard_map.60 = f32[136,256]{1,0:T(8,128)S(1)} custom-call(s32[2,3072]{1,0:T(2,128)S(1)} %pad_add_fusion.pick_ref, bf16[3072,128]{1,0:T(8,128)(2,1)S(1)} %constant_dynamic-slice_fusion.feats_ref, f32[8,16,256]{2,1,0:T(8,128)S(1)} %copy-done.6, bf16[128,512]{1,0:T(8,128)(2,1)S(1)} %get-tuple-element.27.refs_0_, ...), custom_call_target="tpu_custom_call" | custom-call | flops 6442450944 | bytes 917504 | tf_op jit(solution)/shard_map/pallas_call | solution.py:335
  76.9 1.6 %collective-permute-start.17 = (f32[136,256]{1,0:T(8,128)S(1)}, f32[136,256]{1,0:T(8,128)S(1)}, u32[]{:S(2)}, u32[]{:S(2)}) collective-permute-start(f32[136,256]{1,0:T(8,128)S(1)} %shard_map.60), channel_id=1, source_target_pairs={{0,16},{8,24},{16,0},{24,8},{1,17},{9,25},{17,1},{25,9},{2,18},{10... | collective-permute-start | bytes 417800 | tf_op jit(solution)/shard_map/ppermute | solution.py:20
  78.5 1.2 %collective-permute-start.18 = (f32[136,256]{1,0:T(8,128)S(1)}, f32[136,256]{1,0:T(8,128)S(1)}, u32[]{:S(2)}, u32[]{:S(2)}) collective-permute-start(f32[136,256]{1,0:T(8,128)S(1)} %shard_map.60), channel_id=1, source_target_pairs={{0,24},{8,16},{16,8},{24,0},{1,25},{9,17},{17,9},{25,1},{2,26},{10... | collective-permute-start | bytes 417800 | tf_op jit(solution)/shard_map/ppermute | solution.py:20
  79.7 0.8 collective-permute-start.16
  80.5 1.2 %collective-permute-start.6 = (s16[128,1152]{1,0:T(8,128)(2,1)S(1)}, s16[128,1152]{1,0:T(8,128)(2,1)S(1)}, u32[]{:S(2)}, u32[]{:S(2)}) collective-permute-start(s16[128,1152]{1,0:T(8,128)(2,1)S(1)} %update_part.1.refs_0_.refs_9_), channel_id=1, source_target_pairs={{0,8},{8,0},{16,24},{24,16},{1,9},{9,1},{17,25},{25,17},{2,10},{10... | collective-permute-start | bytes 884744 | tf_op jit(solution)/shard_map/ppermute | solution.py:20
  81.7 0.8 collective-permute-start.7
  82.5 3.6 %collective-permute-done.17 = f32[136,256]{1,0:T(8,128)S(1)} collective-permute-done((f32[136,256]{1,0:T(8,128)S(1)}, f32[136,256]{1,0:T(8,128)S(1)}, u32[]{:S(2)}, u32[]{:S(2)}) %collective-permute-start.17) | collective-permute-done | bytes 139296 | tf_op jit(solution)/shard_map/ppermute | solution.py:20
  86.1 1.5 %collective-permute-start.8 = (s16[128,1152]{1,0:T(8,128)(2,1)S(1)}, s16[128,1152]{1,0:T(8,128)(2,1)S(1)}, u32[]{:S(2)}, u32[]{:S(2)}) collective-permute-start(s16[128,1152]{1,0:T(8,128)(2,1)S(1)} %update_part.1.refs_0_.refs_9_), channel_id=1, source_target_pairs={{0,24},{8,16},{16,8},{24,0},{1,25},{9,17},{17,9},{25,1},{2,26},{10... | collective-permute-start | bytes 884744 | tf_op jit(solution)/shard_map/ppermute | solution.py:20
  87.6 0.0 collective-permute-done.18
  87.6 0.4 collective-permute-done.16
  88.1 0.7 add_divide_fusion
  88.8 5.6 %collective-permute-done.6.refs_1_ = s16[128,1152]{1,0:T(8,128)(2,1)S(1)} collective-permute-done((s16[128,1152]{1,0:T(8,128)(2,1)S(1)}, s16[128,1152]{1,0:T(8,128)(2,1)S(1)}, u32[]{:S(2)}, u32[]{:S(2)}) %collective-permute-start.6) | collective-permute-done | bytes 294944 | tf_op jit(solution)/shard_map/ppermute | solution.py:20
  94.3 0.0 collective-permute-done.7.refs_2_
  94.3 5.1 %collective-permute-done.8.refs_3_ = s16[128,1152]{1,0:T(8,128)(2,1)S(1)} collective-permute-done((s16[128,1152]{1,0:T(8,128)(2,1)S(1)}, s16[128,1152]{1,0:T(8,128)(2,1)S(1)}, u32[]{:S(2)}, u32[]{:S(2)}) %collective-permute-start.8) | collective-permute-done | bytes 294944 | tf_op jit(solution)/shard_map/ppermute | solution.py:20
  99.4 2.1 %join_parts.1 = f32[512,1024]{1,0:T(8,128)} custom-call(s32[1]{0:T(128)} %bitcast.pos_ref, s16[128,1152]{1,0:T(8,128)(2,1)S(1)} %update_part.1.refs_0_.refs_9_, s16[128,1152]{1,0:T(8,128)(2,1)S(1)} %collective-permute-done.6.refs_1_, s16[128,1152]{1,0:T(8,128)(2,1)S(1)} %collective-permute-done.7.refs_2_, s16[128,1152]{1,0:T(8,128)(2,1)S(1)} %collective-permute-done.8.refs_3_), custom_call_target="tpu_custom_call" | custom-call | tf_op jit(solution)/shard_map/join_parts/pallas_call | solution.py:236
  (11 shorter events, 0.3 us)
Async XLA Ops:
  0.6 2.8 %copy-start = (bf16[3072,1024]{1,0:T(8,128)(2,1)S(1)}, bf16[3072,1024]{1,0:T(8,128)(2,1)}, u32[]{:S(2)}) copy-start(bf16[3072,1024]{1,0:T(8,128)(2,1)} %rows_ref.3) | copy-start | bytes 18874372
  3.4 1.2 %copy-start.4 = (bf16[512,1024]{1,0:T(8,128)(2,1)S(1)}, bf16[512,1024]{1,0:T(8,128)(2,1)}, u32[]{:S(2)}) copy-start(bf16[512,1024]{1,0:T(8,128)(2,1)} %cent_ref.5) | copy-start | bytes 3145732
  4.6 8.7 %copy-start.5 = (bf16[512,1024]{1,0:T(8,128)(2,1)S(1)}, bf16[512,1024]{1,0:T(8,128)(2,1)}, u32[]{:S(2)}) copy-start(bf16[512,1024]{1,0:T(8,128)(2,1)} %cent_ref.5) | copy-start | bytes 3145732
  4.6 17.0 %copy-start.7 = (s32[3072]{0:T(1024)S(1)}, s32[3072]{0:T(1024)}, u32[]{:S(2)}) copy-start(s32[3072]{0:T(1024)} %param.5) | copy-start | bytes 36868
  10.2 2.6 %copy-start.2 = (f32[512,3072]{1,0:T(8,128)}, f32[512,3072]{1,0:T(8,128)S(1)}, u32[]{:S(2)}) copy-start(f32[512,3072]{1,0:T(8,128)S(1)} %get-tuple-element.20.logits_ref) | copy-start | bytes 18874372
  12.9 8.6 %collective-permute-start = (f32[2,3072]{1,0:T(2,128)S(1)}, f32[2,3072]{1,0:T(2,128)S(1)}, u32[]{:S(2)}, u32[]{:S(2)}) collective-permute-start(f32[2,3072]{1,0:T(2,128)S(1)} %get-tuple-element.21), channel_id=1, source_target_pairs={{0,1},{1,0},{2,3},{3,2},{4,5},{5,4},{6,7},{7,6},{8,9},{9,8},{10,11... | collective-permute-start | bytes 73736 | tf_op jit(solution)/shard_map/ppermute | solution.py:20
  13.8 20.7 %collective-permute-start.10 = (bf16[128,512]{1,0:T(8,128)(2,1)S(1)}, bf16[128,512]{1,0:T(8,128)(2,1)S(1)}, u32[]{:S(2)}, u32[]{:S(2)}) collective-permute-start(bf16[128,512]{1,0:T(8,128)(2,1)S(1)} %get-tuple-element.30), channel_id=1, source_target_pairs={{0,2},{1,3},{2,0},{3,1},{4,6},{5,7},{6,4},{7,5},{8,10},{9,11},{10,... | collective-permute-start | bytes 393224 | tf_op jit(solution)/shard_map/ppermute | solution.py:20
  16.4 21.0 %collective-permute-start.11 = (bf16[128,512]{1,0:T(8,128)(2,1)S(1)}, bf16[128,512]{1,0:T(8,128)(2,1)S(1)}, u32[]{:S(2)}, u32[]{:S(2)}) collective-permute-start(bf16[128,512]{1,0:T(8,128)(2,1)S(1)} %get-tuple-element.31), channel_id=1, source_target_pairs={{0,3},{1,2},{2,1},{3,0},{4,7},{5,6},{6,5},{7,4},{8,11},{9,10},{10,... | collective-permute-start | bytes 393224 | tf_op jit(solution)/shard_map/ppermute | solution.py:20
  16.6 32.3 %collective-permute-start.14 = (bf16[128,512]{1,0:T(8,128)(2,1)S(1)}, bf16[128,512]{1,0:T(8,128)(2,1)S(1)}, u32[]{:S(2)}, u32[]{:S(2)}) collective-permute-start(bf16[128,512]{1,0:T(8,128)(2,1)S(1)} %get-tuple-element.36), channel_id=1, source_target_pairs={{0,6},{1,7},{2,4},{3,5},{4,2},{5,3},{6,0},{7,1},{8,14},{9,15},{10,... | collective-permute-start | bytes 393224 | tf_op jit(solution)/shard_map/ppermute | solution.py:20
  20.3 30.2 %collective-permute-start.15 = (bf16[128,512]{1,0:T(8,128)(2,1)S(1)}, bf16[128,512]{1,0:T(8,128)(2,1)S(1)}, u32[]{:S(2)}, u32[]{:S(2)}) collective-permute-start(bf16[128,512]{1,0:T(8,128)(2,1)S(1)} %get-tuple-element.37), channel_id=1, source_target_pairs={{0,7},{1,6},{2,5},{3,4},{4,3},{5,2},{6,1},{7,0},{8,15},{9,14},{10,... | collective-permute-start | bytes 393224 | tf_op jit(solution)/shard_map/ppermute | solution.py:20
  21.6 7.2 %collective-permute-start.1 = (f32[2,3072]{1,0:T(2,128)S(1)}, f32[2,3072]{1,0:T(2,128)S(1)}, u32[]{:S(2)}, u32[]{:S(2)}) collective-permute-start(f32[2,3072]{1,0:T(2,128)S(1)} %pad_maximum_fusion), channel_id=1, source_target_pairs={{0,2},{1,3},{2,0},{3,1},{4,6},{5,7},{6,4},{7,5},{8,10},{9,11},{10,... | collective-permute-start | bytes 73736 | tf_op jit(solution)/shard_map/ppermute | solution.py:20
  28.9 5.3 %collective-permute-start.2 = (f32[2,3072]{1,0:T(2,128)S(1)}, f32[2,3072]{1,0:T(2,128)S(1)}, u32[]{:S(2)}, u32[]{:S(2)}) collective-permute-start(f32[2,3072]{1,0:T(2,128)S(1)} %pad_maximum_fusion.1), channel_id=1, source_target_pairs={{0,4},{1,5},{2,6},{3,7},{4,0},{5,1},{6,2},{7,3},{8,12},{9,13},{10,... | collective-permute-start | bytes 73736 | tf_op jit(solution)/shard_map/ppermute | solution.py:20
  34.4 17.6 %collective-permute-start.9 = (bf16[128,512]{1,0:T(8,128)(2,1)S(1)}, bf16[128,512]{1,0:T(8,128)(2,1)S(1)}, u32[]{:S(2)}, u32[]{:S(2)}) collective-permute-start(bf16[128,512]{1,0:T(8,128)(2,1)S(1)} %get-tuple-element.29), channel_id=1, source_target_pairs={{0,1},{1,0},{2,3},{3,2},{4,5},{5,4},{6,7},{7,6},{8,9},{9,8},{10,11... | collective-permute-start | bytes 393224 | tf_op jit(solution)/shard_map/ppermute | solution.py:20
  34.4 18.0 %collective-permute-start.12 = (bf16[128,512]{1,0:T(8,128)(2,1)S(1)}, bf16[128,512]{1,0:T(8,128)(2,1)S(1)}, u32[]{:S(2)}, u32[]{:S(2)}) collective-permute-start(bf16[128,512]{1,0:T(8,128)(2,1)S(1)} %get-tuple-element.33), channel_id=1, source_target_pairs={{0,4},{1,5},{2,6},{3,7},{4,0},{5,1},{6,2},{7,3},{8,12},{9,13},{10,... | collective-permute-start | bytes 393224 | tf_op jit(solution)/shard_map/ppermute | solution.py:20
  37.5 15.0 %collective-permute-start.13 = (bf16[128,512]{1,0:T(8,128)(2,1)S(1)}, bf16[128,512]{1,0:T(8,128)(2,1)S(1)}, u32[]{:S(2)}, u32[]{:S(2)}) collective-permute-start(bf16[128,512]{1,0:T(8,128)(2,1)S(1)} %get-tuple-element.35), channel_id=1, source_target_pairs={{0,5},{1,4},{2,7},{3,6},{4,1},{5,0},{6,3},{7,2},{8,13},{9,12},{10,... | collective-permute-start | bytes 393224 | tf_op jit(solution)/shard_map/ppermute | solution.py:20
  37.6 2.8 %copy-start.1 = (bf16[3072,1024]{1,0:T(8,128)(2,1)S(1)}, bf16[3072,1024]{1,0:T(8,128)(2,1)}, u32[]{:S(2)}) copy-start(bf16[3072,1024]{1,0:T(8,128)(2,1)} %rows_ref.3) | copy-start | bytes 18874372
  40.3 2.8 %copy-start.3 = (f32[512,3072]{1,0:T(8,128)S(1)}, f32[512,3072]{1,0:T(8,128)}, u32[]{:S(2)}) copy-start(f32[512,3072]{1,0:T(8,128)} %copy-done.2) | copy-start | bytes 18874372
  43.1 9.4 %copy-start.6 = (f32[8,16,256]{2,1,0:T(8,128)S(1)}, f32[8,16,256]{2,1,0:T(8,128)}, u32[]{:S(2)}) copy-start(f32[8,16,256]{2,1,0:T(8,128)} %code_ref.3) | copy-start | bytes 393220
  48.9 13.9 %collective-permute-start.3 = (s16[128,1152]{1,0:T(8,128)(2,1)S(1)}, s16[128,1152]{1,0:T(8,128)(2,1)S(1)}, u32[]{:S(2)}, u32[]{:S(2)}) collective-permute-start(s16[128,1152]{1,0:T(8,128)(2,1)S(1)} %get-tuple-element.24), channel_id=1, source_target_pairs={{0,8},{8,0},{16,24},{24,16},{1,9},{9,1},{17,25},{25,17},{2,10},{10... | collective-permute-start | bytes 884744 | tf_op jit(solution)/shard_map/ppermute | solution.py:20
  50.5 15.1 %collective-permute-start.4 = (s16[128,1152]{1,0:T(8,128)(2,1)S(1)}, s16[128,1152]{1,0:T(8,128)(2,1)S(1)}, u32[]{:S(2)}, u32[]{:S(2)}) collective-permute-start(s16[128,1152]{1,0:T(8,128)(2,1)S(1)} %get-tuple-element.25), channel_id=1, source_target_pairs={{0,16},{8,24},{16,0},{24,8},{1,17},{9,25},{17,1},{25,9},{2,18},{10... | collective-permute-start | bytes 884744 | tf_op jit(solution)/shard_map/ppermute | solution.py:20
  52.0 13.6 %collective-permute-start.5 = (s16[128,1152]{1,0:T(8,128)(2,1)S(1)}, s16[128,1152]{1,0:T(8,128)(2,1)S(1)}, u32[]{:S(2)}, u32[]{:S(2)}) collective-permute-start(s16[128,1152]{1,0:T(8,128)(2,1)S(1)} %get-tuple-element.26), channel_id=1, source_target_pairs={{0,24},{8,16},{16,8},{24,0},{1,25},{9,17},{17,9},{25,1},{2,26},{10... | collective-permute-start | bytes 884744 | tf_op jit(solution)/shard_map/ppermute | solution.py:20
  76.9 9.2 %collective-permute-start.17 = (f32[136,256]{1,0:T(8,128)S(1)}, f32[136,256]{1,0:T(8,128)S(1)}, u32[]{:S(2)}, u32[]{:S(2)}) collective-permute-start(f32[136,256]{1,0:T(8,128)S(1)} %shard_map.60), channel_id=1, source_target_pairs={{0,16},{8,24},{16,0},{24,8},{1,17},{9,25},{17,1},{25,9},{2,18},{10... | collective-permute-start | bytes 417800 | tf_op jit(solution)/shard_map/ppermute | solution.py:20
  78.5 9.1 %collective-permute-start.18 = (f32[136,256]{1,0:T(8,128)S(1)}, f32[136,256]{1,0:T(8,128)S(1)}, u32[]{:S(2)}, u32[]{:S(2)}) collective-permute-start(f32[136,256]{1,0:T(8,128)S(1)} %shard_map.60), channel_id=1, source_target_pairs={{0,24},{8,16},{16,8},{24,0},{1,25},{9,17},{17,9},{25,1},{2,26},{10... | collective-permute-start | bytes 417800 | tf_op jit(solution)/shard_map/ppermute | solution.py:20
  79.7 8.3 %collective-permute-start.16 = (f32[136,256]{1,0:T(8,128)S(1)}, f32[136,256]{1,0:T(8,128)S(1)}, u32[]{:S(2)}, u32[]{:S(2)}) collective-permute-start(f32[136,256]{1,0:T(8,128)S(1)} %shard_map.60), channel_id=1, source_target_pairs={{0,8},{8,0},{16,24},{24,16},{1,9},{9,1},{17,25},{25,17},{2,10},{10... | collective-permute-start | bytes 417800 | tf_op jit(solution)/shard_map/ppermute | solution.py:20
  80.5 13.8 %collective-permute-start.6 = (s16[128,1152]{1,0:T(8,128)(2,1)S(1)}, s16[128,1152]{1,0:T(8,128)(2,1)S(1)}, u32[]{:S(2)}, u32[]{:S(2)}) collective-permute-start(s16[128,1152]{1,0:T(8,128)(2,1)S(1)} %update_part.1.refs_0_.refs_9_), channel_id=1, source_target_pairs={{0,8},{8,0},{16,24},{24,16},{1,9},{9,1},{17,25},{25,17},{2,10},{10... | collective-permute-start | bytes 884744 | tf_op jit(solution)/shard_map/ppermute | solution.py:20
  81.7 12.6 %collective-permute-start.7 = (s16[128,1152]{1,0:T(8,128)(2,1)S(1)}, s16[128,1152]{1,0:T(8,128)(2,1)S(1)}, u32[]{:S(2)}, u32[]{:S(2)}) collective-permute-start(s16[128,1152]{1,0:T(8,128)(2,1)S(1)} %update_part.1.refs_0_.refs_9_), channel_id=1, source_target_pairs={{0,16},{8,24},{16,0},{24,8},{1,17},{9,25},{17,1},{25,9},{2,18},{10... | collective-permute-start | bytes 884744 | tf_op jit(solution)/shard_map/ppermute | solution.py:20
  86.1 13.3 %collective-permute-start.8 = (s16[128,1152]{1,0:T(8,128)(2,1)S(1)}, s16[128,1152]{1,0:T(8,128)(2,1)S(1)}, u32[]{:S(2)}, u32[]{:S(2)}) collective-permute-start(s16[128,1152]{1,0:T(8,128)(2,1)S(1)} %update_part.1.refs_0_.refs_9_), channel_id=1, source_target_pairs={{0,24},{8,16},{16,8},{24,0},{1,25},{9,17},{17,9},{25,1},{2,26},{10... | collective-permute-start | bytes 884744 | tf_op jit(solution)/shard_map/ppermute | solution.py:20
where the time goes:
time: 102 us
  Pallas kernels  35.6 us (35%)
  waiting for transfers between devices  26.2 us (26%)
  starting transfers between devices  24.5 us (24%)
  local copies, waits for them, and re-layouts  13.4 us (13%)
    ppermute x19, waiting for transfers between devices, swap(): return lax.ppermute(value, axis, [(i, i ^ hop) for i in range(size)])  26.2 us
    ppermute x19, starting transfers between devices, swap(): return lax.ppermute(value, axis, [(i, i ^ hop) for i in range(size)])  24.5 us
    pallas_call x2, Pallas kernels, local_codes(): pl.pallas_call(functools.partial(codes_kernel, peers=peers, half=half), g...  20.5 us
    unnamed x16, local copies, waits for them, and re-layouts  12.2 us
    pallas_call x1, Pallas kernels, local_sums(): pl.pallas_call(functools.partial(sums_kernel, peers=peers), grid=(rows //...  5.77 us
    pallas_call x1, Pallas kernels, local_logits(): pl.pallas_call(logits_kernel, grid=(rows // block,), out_shape=[jax.Shape...  5.59 us
    pallas_call x1, Pallas kernels, join_parts(): pl.pallas_call(join_kernel, out_shape=jax.ShapeDtypeStruct((size * len(co...  2.14 us
  transfers between devices with their start and end apart: 19, of which 7 were waited for; matrix products, arithmetic and copies ran while one was open for 2% of the time, Pallas kernels for 16%

commit v1 on v0

--- a/solution.py
+++ b/solution.py
@@ -80,45 +80,64 @@
     )(position, centroids)
 
 
-def logits_kernel(cent_ref, rows_ref, logits_ref, stats_ref, half_ref):
-    @pl.when(pl.program_id(0) == 0)
-    def _():
-        wide = cent_ref[...].astype(F32)
-        half_ref[...] = jnp.broadcast_to(
-            0.5 * jnp.sum(wide * wide, axis=1, keepdims=True), half_ref.shape
+def spans(rows):
+    short = block_of(rows, 512)
+    cuts = [0, short] if rows > short else [0]
+    while rows - cuts[-1] > 2 * short:
+        cuts.append(cuts[-1] + 2 * short)
+    if rows - cuts[-1] > short:
+        cuts.append(cuts[-1] + short)
+    return list(zip(cuts, cuts[1:] + [rows]))
+
+
+def logits_kernel(cent_hbm, rows_hbm, logits_hbm, stats_ref, cent_ref, rows_ref, logits_ref, in_sem, out_sem):
+    parts = spans(rows_hbm.shape[0])
+    copies = [pltpu.make_async_copy(cent_hbm, cent_ref, in_sem.at[len(parts)])]
+    copies += [
+        pltpu.make_async_copy(rows_hbm.at[lo:hi], rows_ref.at[lo:hi], in_sem.at[at])
+        for at, (lo, hi) in enumerate(parts)
+    ]
+    for copy in copies:
+        copy.start()
+    copies[0].wait()
+    wide = cent_ref[...].astype(F32)
+    half = 0.5 * jnp.sum(wide * wide, axis=1, keepdims=True)
+    outs = []
+    for at, (lo, hi) in enumerate(parts):
+        copies[1 + at].wait()
+        logits = (
+            lax.dot_general(cent_ref[...], rows_ref[lo:hi, :], NT, preferred_element_type=F32) - half
         )
-
-    logits = (
-        lax.dot_general(cent_ref[...], rows_ref[...], NT, preferred_element_type=F32)
-        - half_ref[:, 0:1]
-    )
-    logits_ref[...] = logits
-    peak = jnp.max(logits, axis=0, keepdims=True)
-    stats_ref[0:1, :] = peak
-    stats_ref[1:2, :] = jnp.sum(jnp.exp(logits - peak), axis=0, keepdims=True)
+        logits_ref[:, lo:hi] = logits
+        outs.append(pltpu.make_async_copy(logits_ref.at[:, lo:hi], logits_hbm.at[:, lo:hi], out_sem.at[at]))
+        outs[-1].start()
+        peak = jnp.max(logits, axis=0, keepdims=True)
+        stats_ref[0:1, lo:hi] = peak
+        stats_ref[1:2, lo:hi] = jnp.sum(jnp.exp(logits - peak), axis=0, keepdims=True)
+    for out in outs:
+        out.wait()
 
 
 def local_logits(centroids, embeddings):
     local_k, feat = centroids.shape
     rows = embeddings.shape[0]
-    block = block_of(rows, 1024)
+    parts = len(spans(rows))
     return pl.pallas_call(
         logits_kernel,
-        grid=(rows // block,),
         out_shape=[
             jax.ShapeDtypeStruct((local_k, rows), F32),
             jax.ShapeDtypeStruct((2, rows), F32),
         ],
-        in_specs=[
-            pl.BlockSpec((local_k, feat), lambda i: (0, 0)),
-            pl.BlockSpec((block, feat), lambda i: (i, 0)),
+        in_specs=[pl.BlockSpec(memory_space=pltpu.HBM)] * 2,
+        out_specs=[pl.BlockSpec(memory_space=pltpu.HBM), pl.BlockSpec(memory_space=VMEM)],
+        scratch_shapes=[
+            VMEM((local_k, feat), BF16),
+            VMEM((rows, feat), BF16),
+            VMEM((local_k, rows), F32),
+            pltpu.SemaphoreType.DMA((parts + 1,)),
+            pltpu.SemaphoreType.DMA((parts,)),
         ],
-        out_specs=[
-            pl.BlockSpec((local_k, block), lambda i: (0, i)),
-            pl.BlockSpec((2, block), lambda i: (0, i)),
-        ],
-        scratch_shapes=[VMEM((local_k, 128), F32)],
-        compiler_params=params(),
+        compiler_params=params(54 << 20),
         cost_estimate=pl.CostEstimate(
             flops=2 * local_k * rows * feat,
             transcendentals=local_k * rows,
@@ -134,60 +153,62 @@
     return jnp.concatenate([peak, total], axis=0)
 
 
-def sums_kernel(pos_ref, logits_ref, stats_ref, rows_ref, *refs, peers):
-    own_ref, own_count_ref = refs[:2]
-    outs, (acc_ref, count_ref) = refs[2 : peers + 1], refs[peers + 1 :]
-    step = pl.program_id(0)
-    probability = jnp.exp(logits_ref[...] - stats_ref[0:1, :]) * (1.0 / stats_ref[1:2, :])
-    partial = probability[:, 0:128]
-    for lane in range(128, probability.shape[1], 128):
-        partial = partial + probability[:, lane : lane + 128]
-    sums = jnp.dot(probability.astype(BF16), rows_ref[...], preferred_element_type=F32)
-
-    @pl.when(step == 0)
-    def _():
-        acc_ref[...] = sums
-        count_ref[...] = partial
-
-    @pl.when(step > 0)
-    def _():
-        acc_ref[...] += sums
-        count_ref[...] += partial
-
-    @pl.when(step == pl.num_programs(0) - 1)
-    def _():
-        part = own_ref.shape[0]
-        for hop in range(peers):
-            start = pl.multiple_of((pos_ref[0] ^ hop) * part, part)
-            count = jnp.sum(count_ref[pl.ds(start, part), :], axis=1, keepdims=True)
-            if hop == 0:
-                own_ref[...] = acc_ref[pl.ds(start, part), :]
-                own_count_ref[...] = jnp.broadcast_to(count, own_count_ref.shape)
-            else:
-                encode(acc_ref[pl.ds(start, part), :], count, outs[hop - 1])
+def sums_kernel(pos_ref, logits_hbm, stats_ref, rows_hbm, own_ref, own_count_ref, *refs, peers):
+    outs, (acc_ref, rows_ref, logits_ref, sem) = refs[: peers - 1], refs[peers - 1 :]
+    parts = spans(rows_hbm.shape[0])
+    copies = [
+        (
+            pltpu.make_async_copy(logits_hbm.at[:, lo:hi], logits_ref.at[:, lo:hi], sem.at[0, at]),
+            pltpu.make_async_copy(rows_hbm.at[lo:hi], rows_ref.at[lo:hi], sem.at[1, at]),
+        )
+        for at, (lo, hi) in enumerate(parts)
+    ]
+    for pair in copies:
+        for copy in pair:
+            copy.start()
+    count = None
+    for (lo, hi), pair in zip(parts, copies):
+        for copy in pair:
+            copy.wait()
+        probability = jnp.exp(logits_ref[:, lo:hi] - stats_ref[0:1, lo:hi]) * (1.0 / stats_ref[1:2, lo:hi])
+        for lane in range(0, hi - lo, 128):
+            piece = probability[:, lane : lane + 128]
+            count = piece if count is None else count + piece
+        sums = jnp.dot(probability.astype(BF16), rows_ref[lo:hi, :], preferred_element_type=F32)
+        if lo == 0:
+            acc_ref[...] = sums
+        else:
+            acc_ref[...] += sums
+    part = own_ref.shape[0]
+    logits_ref[:, 0:128] = jnp.broadcast_to(jnp.sum(count, axis=1, keepdims=True), count.shape)
+    for hop in range(peers):
+        start = pl.multiple_of((pos_ref[0] ^ hop) * part, part)
+        total, weight = acc_ref[pl.ds(start, part), :], logits_ref[pl.ds(start, part), 0:128]
+        if hop == 0:
+            own_ref[...] = total
+            own_count_ref[...] = weight
+        else:
+            encode(total, weight, outs[hop - 1])
 
 
 def local_sums(position, logits, stats, embeddings, peers):
     local_k, rows = logits.shape
     feat = embeddings.shape[1]
-    block = block_of(rows, 1024)
     part = local_k // peers
-    whole = lambda shape: pl.BlockSpec(shape, lambda i: (0, 0))
+    in_vmem, in_hbm = pl.BlockSpec(memory_space=VMEM), pl.BlockSpec(memory_space=pltpu.HBM)
     return pl.pallas_call(
         functools.partial(sums_kernel, peers=peers),
-        grid=(rows // block,),
         out_shape=[jax.ShapeDtypeStruct((part, feat), F32), jax.ShapeDtypeStruct((part, 128), F32)]
         + [jax.ShapeDtypeStruct((part, feat + 128), jnp.int16)] * (peers - 1),
-        in_specs=[
-            pl.BlockSpec(memory_space=SMEM),
-            pl.BlockSpec((local_k, block), lambda i: (0, i)),
-            pl.BlockSpec((2, block), lambda i: (0, i)),
-            pl.BlockSpec((block, feat), lambda i: (i, 0)),
+        in_specs=[pl.BlockSpec(memory_space=SMEM), in_hbm, in_vmem, in_hbm],
+        out_specs=[in_vmem] * (peers + 1),
+        scratch_shapes=[
+            VMEM((local_k, feat), F32),
+            VMEM((rows, feat), BF16),
+            VMEM((local_k, rows), F32),
+            pltpu.SemaphoreType.DMA((2, len(spans(rows)))),
         ],
-        out_specs=[whole((part, feat)), whole((part, 128))]
-        + [whole((part, feat + 128))] * (peers - 1),
-        scratch_shapes=[VMEM((local_k, feat), F32), VMEM((local_k, 128), F32)],
-        compiler_params=params(),
+        compiler_params=params(50 << 20),
         cost_estimate=pl.CostEstimate(
             flops=2 * local_k * rows * feat,
             transcendentals=local_k * rows,
@@ -251,33 +272,33 @@
     return first, second, third
 
 
-def codes_kernel(pick_ref, feats_ref, code_ref, *refs, peers, half):
+def codes_kernel(pick_ref, feats_ref, code_ref, *refs, peers, first, last):
     former = refs[peers : peers + 1]
     refs = refs[:peers] + refs[-5:]
     tables, (out_ref, table_ref, weight_ref, data_ref, acc_ref) = refs[:peers], refs[peers:]
     step = pl.program_id(0)
-    groups, sub_dim, words = code_ref.shape
-    width, local_k = tables[0].shape
-    first_feat = half * width
+    groups, sub_dim, words = last - first, *code_ref.shape[1:]
+    width, local_k = groups * sub_dim, tables[0].shape[1]
+    first_feat = first * sub_dim
     block = feats_ref.shape[0]
     head = 3 * sub_dim
 
     @pl.when(step == 0)
     def _():
         for hop in range(peers):
-            table_ref[hop * width : (hop + 1) * width, :] = tables[hop][...]
+            table_ref[hop * width : (hop + 1) * width, :] = tables[hop][first_feat : first_feat + width, :]
         scale = 1.0 / math.log(2.0)
         lane_row = lax.broadcasted_iota(jnp.int32, (sub_dim, words), 0)
         for group in range(groups):
-            code = code_ref[group]
-            first, second, third = three_terms(code * scale)
+            code = code_ref[first + group]
+            one, two, three = three_terms(code * scale)
             half = -0.5 * scale * jnp.sum(code * code, axis=0, keepdims=True)
             bias = [jnp.broadcast_to(t.astype(F32), (sub_dim, words)) for t in three_terms(half)]
             bias = jnp.where(
                 lane_row == 0, bias[0], jnp.where(lane_row == 1, bias[1], jnp.where(lane_row == 2, bias[2], 0.0))
             )
-            first, second, third = (t.astype(F32) for t in (first, second, third))
-            stacked = jnp.concatenate([first, first, bias, second, second, third, third], axis=0)
+            one, two, three = (t.astype(F32) for t in (one, two, three))
+            stacked = jnp.concatenate([one, one, bias, two, two, three, three], axis=0)
             weight_ref[group * words : (group + 1) * words, :] = stacked.T.astype(BF16)
         acc_ref[...] = jnp.zeros_like(acc_ref)
         for group in range(groups):
@@ -311,40 +332,42 @@
 
     @pl.when(step == pl.num_programs(0) - 1)
     def _():
-        if half:
-            out_ref[0 : former[0].shape[0], :] = former[0][...]
-        first_row, first_count = half * groups * sub_dim, out_ref.shape[0] - (half + 1) * groups
-        if half:
-            out_ref[first_count + groups :, :] = former[0][half * groups * sub_dim :, :]
+        counts = last * sub_dim
+        if first:
+            out_ref[0:first_feat, :] = former[0][0:first_feat, :]
+            out_ref[counts : counts + first, :] = former[0][first_feat:, :]
         for group in range(groups):
             found = acc_ref[group].T
-            row = first_row + group * sub_dim
+            row = first_feat + group * sub_dim
             out_ref[row : row + sub_dim, :] = found[0:sub_dim] + found[sub_dim : 2 * sub_dim]
-            out_ref[first_count + group : first_count + group + 1, :] = found[2 * sub_dim : 2 * sub_dim + 1]
-
-
-def local_codes(pick, features, codebooks, tables, half, halves, former=(), after=()):
+            out_ref[counts + first + group : counts + first + group + 1, :] = found[
+                2 * sub_dim : 2 * sub_dim + 1
+            ]
+
+
+def local_codes(pick, features, codebooks, tables, first, last, former=(), after=()):
     peers = len(tables)
     rows, feats = features.shape
     local_k = tables[0].shape[1]
-    groups, sub_dim, words = codebooks.shape
-    groups, width = groups // halves, feats // halves
+    sub_dim, words = codebooks.shape[1:]
+    groups = last - first
+    width = groups * sub_dim
     block = block_of(rows, 1536)
     depth = 7 * sub_dim
     fixed = lambda shape: pl.BlockSpec(shape, lambda i: (0,) * len(shape))
     return pl.pallas_call(
-        functools.partial(codes_kernel, peers=peers, half=half),
+        functools.partial(codes_kernel, peers=peers, first=first, last=last),
         grid=(rows // block,),
-        out_shape=jax.ShapeDtypeStruct(((half + 1) * groups * (sub_dim + 1), words), F32),
+        out_shape=jax.ShapeDtypeStruct((last * (sub_dim + 1), words), F32),
         in_specs=[
             pl.BlockSpec((2, block), lambda i: (0, i)),
             pl.BlockSpec((block, feats), lambda i: (i, 0)),
-            pl.BlockSpec((groups, sub_dim, words), lambda i: (half, 0, 0)),
+            fixed(codebooks.shape),
         ]
-        + [pl.BlockSpec((width, local_k), lambda i: (half, 0))] * peers
+        + [fixed((feats, local_k))] * peers
         + [fixed(each.shape) for each in former]
         + [pl.BlockSpec(memory_space=pl.ANY)] * len(after),
-        out_specs=fixed(((half + 1) * groups * (sub_dim + 1), words)),
+        out_specs=fixed((last * (sub_dim + 1), words)),
         scratch_shapes=[
             VMEM((peers * width, local_k), BF16),
             VMEM((groups * words, depth), BF16),
@@ -357,6 +380,7 @@
             transcendentals=rows * groups * words,
             bytes_accessed=rows * width * 2 + peers * width * local_k * 2,
         ),
+        name="local_codes",
     )(pick, features, codebooks, *tables, *former, *after)
 
 
@@ -403,16 +427,16 @@
 
     pick = jnp.stack([(assignment // local_k) ^ sub_at, assignment % local_k]).astype(jnp.int32)
     features = lax.dynamic_slice_in_dim(embeddings, sub_at * width, width, 1)
-    found = local_codes(pick, features, codebooks, tables, 0, 2)
-    found = local_codes(pick, features, codebooks, tables, 1, 2, (found,), (code,))
+    early = (groups * 5 + 7) // 8
+    found = local_codes(pick, features, codebooks, tables, 0, early)
+    found = local_codes(pick, features, codebooks, tables, early, groups, (found,), (code,))
     pieces = [found]
     for hop in hops:
         pieces.append(swap(found, "dp", n_dp, hop))
     while len(pieces) > 1:
         pieces = [pieces[i] + pieces[i + 1] for i in range(0, len(pieces), 2)]
-    total, each = pieces[0], groups // 2
-    code_sums = total[: groups * sub_dim].reshape(groups, sub_dim, words)
-    code_counts = jnp.concatenate([total[groups * sub_dim + each :], total[groups * sub_dim : groups * sub_dim + each]])
+    code_sums = pieces[0][: groups * sub_dim].reshape(groups, sub_dim, words)
+    code_counts = pieces[0][groups * sub_dim :]
     new_codebooks = (code_sums + codebooks) / (code_counts[:, None, :] + 1.0)
     return (new_centroids, new_codebooks)
 

time: 102 us -> 95 us (0.931)
  local copies, waits for them, and re-layouts: 13.4 us -> 1.21 us
  Pallas kernels: 35.6 us -> 39.6 us
  waiting for transfers between devices: 26.2 us -> 27.5 us
    unnamed x16 -> x6, local copies, waits for them, and re-layouts: 12.2 us -> 0.01 us
    pallas_call x4, Pallas kernels: 31.9 us -> 35.8 us  [the longest x2 20.4 us: local_codes(): pl.pallas_call(functools.partial(codes_kernel, peers=peers, first=first,...]
    ppermute x19, waiting for transfers between devices: 26.2 us -> 27.5 us  [swap(): return lax.ppermute(value, axis, [(i, i ^ hop) for i in range(size)])]
  transfers between devices with their start and end apart: 19 -> 19, of which waited for: 7 -> 6; matrix products, arithmetic and copies ran while one was open for 2% -> 3% of each run, Pallas kernels for 16% -> 21%
where the time goes in v1:
time: 95 us; the launch traced here: 94.7 us
  Pallas kernels  39.6 us (42%)
  waiting for transfers between devices  27.5 us (29%)
  starting transfers between devices  23.9 us (25%)
  other arithmetic  1.8 us (2%)
  local copies, waits for them, and re-layouts  1.21 us (1%)
    ppermute x19, waiting for transfers between devices, swap(): return lax.ppermute(value, axis, [(i, i ^ hop) for i in range(size)])  27.5 us
    ppermute x19, starting transfers between devices, swap(): return lax.ppermute(value, axis, [(i, i ^ hop) for i in range(size)])  23.9 us
    pallas_call x2, Pallas kernels, local_codes(): pl.pallas_call(functools.partial(codes_kernel, peers=peers, first=first,...  20.4 us
    pallas_call x1, Pallas kernels, local_logits(): pl.pallas_call(logits_kernel, out_shape=[jax.ShapeDtypeStruct((local_k, r...  8.47 us
    pallas_call x1, Pallas kernels, local_sums(): pl.pallas_call(functools.partial(sums_kernel, peers=peers), out_shape=[ja...  6.96 us
    pallas_call x1, Pallas kernels, join_parts(): pl.pallas_call(join_kernel, out_shape=jax.ShapeDtypeStruct((size * len(co...  2.14 us
  transfers between devices with their start and end apart: 19, of which 6 were waited for; matrix products, arithmetic and copies ran while one was open for 3% of the time, Pallas kernels for 21%

profile of v1, /device:TPU:0, one launch (start us, length us, event | category | flops | bytes accessed | tf_op | source)
XLA Modules:
  0.0 94.7 jit_solution(4617086075542715450)
XLA Ops:
  0.6 0.0 copy-start
  0.6 0.0 copy-start.2
  0.6 8.5 %local_logits.1 = (f32[512,3072]{1,0:T(8,128)}, f32[2,3072]{1,0:T(2,128)}) custom-call(bf16[512,1024]{1,0:T(8,128)(2,1)} %cent_ref.3, bf16[3072,1024]{1,0:T(8,128)(2,1)} %rows_hbm.3), custom_call_target="tpu_custom_call" | custom-call | flops 3221225472 | bytes 12582912 | tf_op jit(solution)/shard_map/local_logits/pallas_call | solution.py:125
  9.1 0.6 collective-permute-start
  9.7 0.0 copy-done
  9.7 0.4 table_parts.1
  10.1 2.7 %collective-permute-start.10 = (bf16[128,512]{1,0:T(8,128)(2,1)S(1)}, bf16[128,512]{1,0:T(8,128)(2,1)S(1)}, u32[]{:S(2)}, u32[]{:S(2)}) collective-permute-start(bf16[128,512]{1,0:T(8,128)(2,1)S(1)} %get-tuple-element.30), channel_id=1, source_target_pairs={{0,2},{1,3},{2,0},{3,1},{4,6},{5,7},{6,4},{7,5},{8,10},{9,11},{10,... | collective-permute-start | bytes 393224 | tf_op jit(solution)/shard_map/ppermute | solution.py:20
  12.7 0.2 collective-permute-start.11
  12.9 3.7 %collective-permute-start.14 = (bf16[128,512]{1,0:T(8,128)(2,1)S(1)}, bf16[128,512]{1,0:T(8,128)(2,1)S(1)}, u32[]{:S(2)}, u32[]{:S(2)}) collective-permute-start(bf16[128,512]{1,0:T(8,128)(2,1)S(1)} %get-tuple-element.36), channel_id=1, source_target_pairs={{0,6},{1,7},{2,4},{3,5},{4,2},{5,3},{6,0},{7,1},{8,14},{9,15},{10,... | collective-permute-start | bytes 393224 | tf_op jit(solution)/shard_map/ppermute | solution.py:20
  16.6 0.0 collective-permute-start.15
  16.6 1.2 %constant_dynamic-slice_fusion.feats_ref = bf16[3072,128]{1,0:T(8,128)(2,1)S(1)} fusion(bf16[3072,1024]{1,0:T(8,128)(2,1)} %rows_hbm.3, s32[]{:T(128)S(6)} %select_n.17), kind=kLoop, calls=%fused_computation.25 | loop fusion | bytes 1572868 | tf_op jit(solution)/shard_map/dynamic_slice | solution.py:429
  17.8 0.0 collective-permute-done
  17.8 0.9 fusion.3
  18.7 0.1 collective-permute-start.1
  18.8 0.0 copy-done.2
  18.8 8.6 %collective-permute-done.1 = f32[2,3072]{1,0:T(2,128)S(1)} collective-permute-done((f32[2,3072]{1,0:T(2,128)S(1)}, f32[2,3072]{1,0:T(2,128)S(1)}, u32[]{:S(2)}, u32[]{:S(2)}) %collective-permute-start.1) | collective-permute-done | bytes 24608 | tf_op jit(solution)/shard_map/ppermute | solution.py:20
  27.5 1.3 %collective-permute-start.2 = (f32[2,3072]{1,0:T(2,128)S(1)}, f32[2,3072]{1,0:T(2,128)S(1)}, u32[]{:S(2)}, u32[]{:S(2)}) collective-permute-start(f32[2,3072]{1,0:T(2,128)S(1)} %pad_maximum_fusion.1), channel_id=1, source_target_pairs={{0,4},{1,5},{2,6},{3,7},{4,0},{5,1},{6,2},{7,3},{8,12},{9,13},{10,... | collective-permute-start | bytes 73736 | tf_op jit(solution)/shard_map/ppermute | solution.py:20
  28.8 3.5 %collective-permute-done.2 = f32[2,3072]{1,0:T(2,128)S(1)} collective-permute-done((f32[2,3072]{1,0:T(2,128)S(1)}, f32[2,3072]{1,0:T(2,128)S(1)}, u32[]{:S(2)}, u32[]{:S(2)}) %collective-permute-start.2) | collective-permute-done | bytes 24608 | tf_op jit(solution)/shard_map/ppermute | solution.py:20
  32.4 0.1 collective-permute-start.9
  32.5 0.0 collective-permute-done.10.refs_2_
  32.5 1.3 %collective-permute-start.12 = (bf16[128,512]{1,0:T(8,128)(2,1)S(1)}, bf16[128,512]{1,0:T(8,128)(2,1)S(1)}, u32[]{:S(2)}, u32[]{:S(2)}) collective-permute-start(bf16[128,512]{1,0:T(8,128)(2,1)S(1)} %get-tuple-element.33), channel_id=1, source_target_pairs={{0,4},{1,5},{2,6},{3,7},{4,0},{5,1},{6,2},{7,3},{8,12},{9,13},{10,... | collective-permute-start | bytes 393224 | tf_op jit(solution)/shard_map/ppermute | solution.py:20
  33.8 0.0 collective-permute-done.11.refs_3_
  33.8 1.5 %collective-permute-start.13 = (bf16[128,512]{1,0:T(8,128)(2,1)S(1)}, bf16[128,512]{1,0:T(8,128)(2,1)S(1)}, u32[]{:S(2)}, u32[]{:S(2)}) collective-permute-start(bf16[128,512]{1,0:T(8,128)(2,1)S(1)} %get-tuple-element.35), channel_id=1, source_target_pairs={{0,5},{1,4},{2,7},{3,6},{4,1},{5,0},{6,3},{7,2},{8,13},{9,12},{10,... | collective-permute-start | bytes 393224 | tf_op jit(solution)/shard_map/ppermute | solution.py:20
  35.2 0.0 copy-start.1
  35.2 7.0 %local_sums.1 = (f32[128,1024]{1,0:T(8,128)S(1)}, f32[128,128]{1,0:T(8,128)S(1)}, s16[128,1152]{1,0:T(8,128)(2,1)S(1)}, s16[128,1152]{1,0:T(8,128)(2,1)S(1)}, s16[128,1152]{1,0:T(8,128)(2,1)S(1)}) custom-call(s32[1]{0:T(128)} %bitcast.pos_ref, f32[512,3072]{1,0:T(8,128)} %get-tuple-element.20.logits_hbm, f32[2,3072]{1,0:T(2,128)S(1)} %pad_maximum_fusion.2.stats_ref, ...), custom_call_target="tpu_custom_call" | custom-call | flops 3221225472 | bytes 12582912 | tf_op jit(solution)/shard_map/local_sums/pallas_call | solution.py:199
  42.2 0.0 collective-permute-done.14.refs_6_
  42.2 1.6 %collective-permute-start.3 = (s16[128,1152]{1,0:T(8,128)(2,1)S(1)}, s16[128,1152]{1,0:T(8,128)(2,1)S(1)}, u32[]{:S(2)}, u32[]{:S(2)}) collective-permute-start(s16[128,1152]{1,0:T(8,128)(2,1)S(1)} %get-tuple-element.24), channel_id=1, source_target_pairs={{0,8},{8,0},{16,24},{24,16},{1,9},{9,1},{17,25},{25,17},{2,10},{10... | collective-permute-start | bytes 884744 | tf_op jit(solution)/shard_map/ppermute | solution.py:20
  43.8 0.0 collective-permute-done.15.refs_7_
  43.8 1.5 %collective-permute-start.4 = (s16[128,1152]{1,0:T(8,128)(2,1)S(1)}, s16[128,1152]{1,0:T(8,128)(2,1)S(1)}, u32[]{:S(2)}, u32[]{:S(2)}) collective-permute-start(s16[128,1152]{1,0:T(8,128)(2,1)S(1)} %get-tuple-element.25), channel_id=1, source_target_pairs={{0,16},{8,24},{16,0},{24,8},{1,17},{9,25},{17,1},{25,9},{2,18},{10... | collective-permute-start | bytes 884744 | tf_op jit(solution)/shard_map/ppermute | solution.py:20
  45.3 0.0 collective-permute-done.9.refs_1_
  45.3 0.5 collective-permute-start.5
  45.8 0.0 collective-permute-done.12.refs_4_
  45.8 1.6 %collective-permute-done.13.refs_5_ = bf16[128,512]{1,0:T(8,128)(2,1)S(1)} collective-permute-done((bf16[128,512]{1,0:T(8,128)(2,1)S(1)}, bf16[128,512]{1,0:T(8,128)(2,1)S(1)}, u32[]{:S(2)}, u32[]{:S(2)}) %collective-permute-start.13) | collective-permute-done | bytes 131104 | tf_op jit(solution)/shard_map/ppermute | solution.py:20
  47.4 0.0 copy-done.1
  47.4 12.6 %local_codes.2.refs_8_ = f32[85,256]{1,0:T(8,128)S(1)} custom-call(s32[2,3072]{1,0:T(2,128)S(1)} %pad_add_fusion.pick_ref, bf16[3072,128]{1,0:T(8,128)(2,1)S(1)} %constant_dynamic-slice_fusion.feats_ref, f32[8,16,256]{2,1,0:T(8,128)S(1)} %copy-done.1, bf16[128,512]{1,0:T(8,128)(2,1)S(1)} %get-tuple-element.27.refs_0_, ...), custom_call_target="tpu_custom_call" | custom-call | flops 8053063680 | bytes 1146880 | tf_op jit(solution)/shard_map/local_codes/pallas_call | solution.py:358
  60.0 0.0 collective-permute-done.3.refs_0_
  60.0 0.0 collective-permute-done.4.refs_1_
  60.0 0.0 collective-permute-done.5.refs_2_
  60.0 1.2 %update_part.1.refs_0_.refs_9_ = s16[128,1152]{1,0:T(8,128)(2,1)S(1)} custom-call(s32[1]{0:T(128)} %bitcast.pos_ref, bf16[512,1024]{1,0:T(8,128)(2,1)S(1)} %copy-done, f32[128,1024]{1,0:T(8,128)S(1)} %get-tuple-element.22.own_ref, f32[128,128]{1,0:T(8,128)S(1)} %get-tuple-element.23.own_count_ref, s16[128,1152]{1,0:T(8,128)(2,1)S(1)} %collective-permute-done.3.refs_0_, ...), custom_call_target="tpu_custom_call" | custom-call | tf_op jit(solution)/shard_map/update_part/pallas_call | solution.py:236
  61.2 7.8 %local_codes.3 = f32[136,256]{1,0:T(8,128)S(1)} custom-call(s32[2,3072]{1,0:T(2,128)S(1)} %pad_add_fusion.pick_ref, bf16[3072,128]{1,0:T(8,128)(2,1)S(1)} %constant_dynamic-slice_fusion.feats_ref, f32[8,16,256]{2,1,0:T(8,128)S(1)} %copy-done.1, bf16[128,512]{1,0:T(8,128)(2,1)S(1)} %get-tuple-element.27.refs_0_, ...), custom_call_target="tpu_custom_call" | custom-call | flops 4831838208 | bytes 688128 | tf_op jit(solution)/shard_map/local_codes/pallas_call | solution.py:358
  69.0 1.6 %collective-permute-start.17 = (f32[136,256]{1,0:T(8,128)S(1)}, f32[136,256]{1,0:T(8,128)S(1)}, u32[]{:S(2)}, u32[]{:S(2)}) collective-permute-start(f32[136,256]{1,0:T(8,128)S(1)} %local_codes.3), channel_id=1, source_target_pairs={{0,16},{8,24},{16,0},{24,8},{1,17},{9,25},{17,1},{25,9},{2,18},{10... | collective-permute-start | bytes 417800 | tf_op jit(solution)/shard_map/ppermute | solution.py:20
  70.6 1.4 %collective-permute-start.18 = (f32[136,256]{1,0:T(8,128)S(1)}, f32[136,256]{1,0:T(8,128)S(1)}, u32[]{:S(2)}, u32[]{:S(2)}) collective-permute-start(f32[136,256]{1,0:T(8,128)S(1)} %local_codes.3), channel_id=1, source_target_pairs={{0,24},{8,16},{16,8},{24,0},{1,25},{9,17},{17,9},{25,1},{2,26},{10... | collective-permute-start | bytes 417800 | tf_op jit(solution)/shard_map/ppermute | solution.py:20
  72.0 0.5 collective-permute-start.16
  72.6 1.5 %collective-permute-start.6 = (s16[128,1152]{1,0:T(8,128)(2,1)S(1)}, s16[128,1152]{1,0:T(8,128)(2,1)S(1)}, u32[]{:S(2)}, u32[]{:S(2)}) collective-permute-start(s16[128,1152]{1,0:T(8,128)(2,1)S(1)} %update_part.1.refs_0_.refs_9_), channel_id=1, source_target_pairs={{0,8},{8,0},{16,24},{24,16},{1,9},{9,1},{17,25},{25,17},{2,10},{10... | collective-permute-start | bytes 884744 | tf_op jit(solution)/shard_map/ppermute | solution.py:20
  74.1 1.5 %collective-permute-start.7 = (s16[128,1152]{1,0:T(8,128)(2,1)S(1)}, s16[128,1152]{1,0:T(8,128)(2,1)S(1)}, u32[]{:S(2)}, u32[]{:S(2)}) collective-permute-start(s16[128,1152]{1,0:T(8,128)(2,1)S(1)} %update_part.1.refs_0_.refs_9_), channel_id=1, source_target_pairs={{0,16},{8,24},{16,0},{24,8},{1,17},{9,25},{17,1},{25,9},{2,18},{10... | collective-permute-start | bytes 884744 | tf_op jit(solution)/shard_map/ppermute | solution.py:20
  75.6 2.9 %collective-permute-done.17 = f32[136,256]{1,0:T(8,128)S(1)} collective-permute-done((f32[136,256]{1,0:T(8,128)S(1)}, f32[136,256]{1,0:T(8,128)S(1)}, u32[]{:S(2)}, u32[]{:S(2)}) %collective-permute-start.17) | collective-permute-done | bytes 139296 | tf_op jit(solution)/shard_map/ppermute | solution.py:20
  78.5 2.5 %collective-permute-start.8 = (s16[128,1152]{1,0:T(8,128)(2,1)S(1)}, s16[128,1152]{1,0:T(8,128)(2,1)S(1)}, u32[]{:S(2)}, u32[]{:S(2)}) collective-permute-start(s16[128,1152]{1,0:T(8,128)(2,1)S(1)} %update_part.1.refs_0_.refs_9_), channel_id=1, source_target_pairs={{0,24},{8,16},{16,8},{24,0},{1,25},{9,17},{17,9},{25,1},{2,26},{10... | collective-permute-start | bytes 884744 | tf_op jit(solution)/shard_map/ppermute | solution.py:20
  81.1 0.0 collective-permute-done.18
  81.1 0.0 collective-permute-done.16
  81.1 0.7 add_divide_fusion
  81.8 4.6 %collective-permute-done.6.refs_1_ = s16[128,1152]{1,0:T(8,128)(2,1)S(1)} collective-permute-done((s16[128,1152]{1,0:T(8,128)(2,1)S(1)}, s16[128,1152]{1,0:T(8,128)(2,1)S(1)}, u32[]{:S(2)}, u32[]{:S(2)}) %collective-permute-start.6) | collective-permute-done | bytes 294944 | tf_op jit(solution)/shard_map/ppermute | solution.py:20
  86.4 0.0 collective-permute-done.7.refs_2_
  86.4 6.2 %collective-permute-done.8.refs_3_ = s16[128,1152]{1,0:T(8,128)(2,1)S(1)} collective-permute-done((s16[128,1152]{1,0:T(8,128)(2,1)S(1)}, s16[128,1152]{1,0:T(8,128)(2,1)S(1)}, u32[]{:S(2)}, u32[]{:S(2)}) %collective-permute-start.8) | collective-permute-done | bytes 294944 | tf_op jit(solution)/shard_map/ppermute | solution.py:20
  92.6 2.1 %join_parts.1 = f32[512,1024]{1,0:T(8,128)} custom-call(s32[1]{0:T(128)} %bitcast.pos_ref, s16[128,1152]{1,0:T(8,128)(2,1)S(1)} %update_part.1.refs_0_.refs_9_, s16[128,1152]{1,0:T(8,128)(2,1)S(1)} %collective-permute-done.6.refs_1_, s16[128,1152]{1,0:T(8,128)(2,1)S(1)} %collective-permute-done.7.refs_2_, s16[128,1152]{1,0:T(8,128)(2,1)S(1)} %collective-permute-done.8.refs_3_), custom_call_target="tpu_custom_call" | custom-call | tf_op jit(solution)/shard_map/join_parts/pallas_call | solution.py:257
  (10 shorter events, 0.3 us)
Async XLA Ops:
  0.6 9.1 %copy-start = (bf16[512,1024]{1,0:T(8,128)(2,1)S(1)}, bf16[512,1024]{1,0:T(8,128)(2,1)}, u32[]{:S(2)}) copy-start(bf16[512,1024]{1,0:T(8,128)(2,1)} %cent_ref.3) | copy-start | bytes 3145732
  0.6 18.2 %copy-start.2 = (s32[3072]{0:T(1024)S(1)}, s32[3072]{0:T(1024)}, u32[]{:S(2)}) copy-start(s32[3072]{0:T(1024)} %param.5) | copy-start | bytes 36868
  9.1 8.7 %collective-permute-start = (f32[2,3072]{1,0:T(2,128)}, f32[2,3072]{1,0:T(2,128)S(1)}, u32[]{:S(2)}, u32[]{:S(2)}) collective-permute-start(f32[2,3072]{1,0:T(2,128)} %get-tuple-element.21), channel_id=1, source_target_pairs={{0,1},{1,0},{2,3},{3,2},{4,5},{5,4},{6,7},{7,6},{8,9},{9,8},{10,11... | collective-permute-start | bytes 73736 | tf_op jit(solution)/shard_map/ppermute | solution.py:20
  10.1 22.4 %collective-permute-start.10 = (bf16[128,512]{1,0:T(8,128)(2,1)S(1)}, bf16[128,512]{1,0:T(8,128)(2,1)S(1)}, u32[]{:S(2)}, u32[]{:S(2)}) collective-permute-start(bf16[128,512]{1,0:T(8,128)(2,1)S(1)} %get-tuple-element.30), channel_id=1, source_target_pairs={{0,2},{1,3},{2,0},{3,1},{4,6},{5,7},{6,4},{7,5},{8,10},{9,11},{10,... | collective-permute-start | bytes 393224 | tf_op jit(solution)/shard_map/ppermute | solution.py:20
  12.7 21.0 %collective-permute-start.11 = (bf16[128,512]{1,0:T(8,128)(2,1)S(1)}, bf16[128,512]{1,0:T(8,128)(2,1)S(1)}, u32[]{:S(2)}, u32[]{:S(2)}) collective-permute-start(bf16[128,512]{1,0:T(8,128)(2,1)S(1)} %get-tuple-element.31), channel_id=1, source_target_pairs={{0,3},{1,2},{2,1},{3,0},{4,7},{5,6},{6,5},{7,4},{8,11},{9,10},{10,... | collective-permute-start | bytes 393224 | tf_op jit(solution)/shard_map/ppermute | solution.py:20
  12.9 29.3 %collective-permute-start.14 = (bf16[128,512]{1,0:T(8,128)(2,1)S(1)}, bf16[128,512]{1,0:T(8,128)(2,1)S(1)}, u32[]{:S(2)}, u32[]{:S(2)}) collective-permute-start(bf16[128,512]{1,0:T(8,128)(2,1)S(1)} %get-tuple-element.36), channel_id=1, source_target_pairs={{0,6},{1,7},{2,4},{3,5},{4,2},{5,3},{6,0},{7,1},{8,14},{9,15},{10,... | collective-permute-start | bytes 393224 | tf_op jit(solution)/shard_map/ppermute | solution.py:20
  16.6 27.2 %collective-permute-start.15 = (bf16[128,512]{1,0:T(8,128)(2,1)S(1)}, bf16[128,512]{1,0:T(8,128)(2,1)S(1)}, u32[]{:S(2)}, u32[]{:S(2)}) collective-permute-start(bf16[128,512]{1,0:T(8,128)(2,1)S(1)} %get-tuple-element.37), channel_id=1, source_target_pairs={{0,7},{1,6},{2,5},{3,4},{4,3},{5,2},{6,1},{7,0},{8,15},{9,14},{10,... | collective-permute-start | bytes 393224 | tf_op jit(solution)/shard_map/ppermute | solution.py:20
  18.7 8.7 %collective-permute-start.1 = (f32[2,3072]{1,0:T(2,128)S(1)}, f32[2,3072]{1,0:T(2,128)S(1)}, u32[]{:S(2)}, u32[]{:S(2)}) collective-permute-start(f32[2,3072]{1,0:T(2,128)S(1)} %pad_maximum_fusion), channel_id=1, source_target_pairs={{0,2},{1,3},{2,0},{3,1},{4,6},{5,7},{6,4},{7,5},{8,10},{9,11},{10,... | collective-permute-start | bytes 73736 | tf_op jit(solution)/shard_map/ppermute | solution.py:20
  27.5 4.8 %collective-permute-start.2 = (f32[2,3072]{1,0:T(2,128)S(1)}, f32[2,3072]{1,0:T(2,128)S(1)}, u32[]{:S(2)}, u32[]{:S(2)}) collective-permute-start(f32[2,3072]{1,0:T(2,128)S(1)} %pad_maximum_fusion.1), channel_id=1, source_target_pairs={{0,4},{1,5},{2,6},{3,7},{4,0},{5,1},{6,2},{7,3},{8,12},{9,13},{10,... | collective-permute-start | bytes 73736 | tf_op jit(solution)/shard_map/ppermute | solution.py:20
  32.4 12.9 %collective-permute-start.9 = (bf16[128,512]{1,0:T(8,128)(2,1)S(1)}, bf16[128,512]{1,0:T(8,128)(2,1)S(1)}, u32[]{:S(2)}, u32[]{:S(2)}) collective-permute-start(bf16[128,512]{1,0:T(8,128)(2,1)S(1)} %get-tuple-element.29), channel_id=1, source_target_pairs={{0,1},{1,0},{2,3},{3,2},{4,5},{5,4},{6,7},{7,6},{8,9},{9,8},{10,11... | collective-permute-start | bytes 393224 | tf_op jit(solution)/shard_map/ppermute | solution.py:20
  32.5 13.3 %collective-permute-start.12 = (bf16[128,512]{1,0:T(8,128)(2,1)S(1)}, bf16[128,512]{1,0:T(8,128)(2,1)S(1)}, u32[]{:S(2)}, u32[]{:S(2)}) collective-permute-start(bf16[128,512]{1,0:T(8,128)(2,1)S(1)} %get-tuple-element.33), channel_id=1, source_target_pairs={{0,4},{1,5},{2,6},{3,7},{4,0},{5,1},{6,2},{7,3},{8,12},{9,13},{10,... | collective-permute-start | bytes 393224 | tf_op jit(solution)/shard_map/ppermute | solution.py:20
  33.8 13.6 %collective-permute-start.13 = (bf16[128,512]{1,0:T(8,128)(2,1)S(1)}, bf16[128,512]{1,0:T(8,128)(2,1)S(1)}, u32[]{:S(2)}, u32[]{:S(2)}) collective-permute-start(bf16[128,512]{1,0:T(8,128)(2,1)S(1)} %get-tuple-element.35), channel_id=1, source_target_pairs={{0,5},{1,4},{2,7},{3,6},{4,1},{5,0},{6,3},{7,2},{8,13},{9,12},{10,... | collective-permute-start | bytes 393224 | tf_op jit(solution)/shard_map/ppermute | solution.py:20
  35.2 12.1 %copy-start.1 = (f32[8,16,256]{2,1,0:T(8,128)S(1)}, f32[8,16,256]{2,1,0:T(8,128)}, u32[]{:S(2)}) copy-start(f32[8,16,256]{2,1,0:T(8,128)} %code_ref.3) | copy-start | bytes 393220
  42.2 17.8 %collective-permute-start.3 = (s16[128,1152]{1,0:T(8,128)(2,1)S(1)}, s16[128,1152]{1,0:T(8,128)(2,1)S(1)}, u32[]{:S(2)}, u32[]{:S(2)}) collective-permute-start(s16[128,1152]{1,0:T(8,128)(2,1)S(1)} %get-tuple-element.24), channel_id=1, source_target_pairs={{0,8},{8,0},{16,24},{24,16},{1,9},{9,1},{17,25},{25,17},{2,10},{10... | collective-permute-start | bytes 884744 | tf_op jit(solution)/shard_map/ppermute | solution.py:20
  43.8 16.2 %collective-permute-start.4 = (s16[128,1152]{1,0:T(8,128)(2,1)S(1)}, s16[128,1152]{1,0:T(8,128)(2,1)S(1)}, u32[]{:S(2)}, u32[]{:S(2)}) collective-permute-start(s16[128,1152]{1,0:T(8,128)(2,1)S(1)} %get-tuple-element.25), channel_id=1, source_target_pairs={{0,16},{8,24},{16,0},{24,8},{1,17},{9,25},{17,1},{25,9},{2,18},{10... | collective-permute-start | bytes 884744 | tf_op jit(solution)/shard_map/ppermute | solution.py:20
  45.3 14.7 %collective-permute-start.5 = (s16[128,1152]{1,0:T(8,128)(2,1)S(1)}, s16[128,1152]{1,0:T(8,128)(2,1)S(1)}, u32[]{:S(2)}, u32[]{:S(2)}) collective-permute-start(s16[128,1152]{1,0:T(8,128)(2,1)S(1)} %get-tuple-element.26), channel_id=1, source_target_pairs={{0,24},{8,16},{16,8},{24,0},{1,25},{9,17},{17,9},{25,1},{2,26},{10... | collective-permute-start | bytes 884744 | tf_op jit(solution)/shard_map/ppermute | solution.py:20
  69.0 9.5 %collective-permute-start.17 = (f32[136,256]{1,0:T(8,128)S(1)}, f32[136,256]{1,0:T(8,128)S(1)}, u32[]{:S(2)}, u32[]{:S(2)}) collective-permute-start(f32[136,256]{1,0:T(8,128)S(1)} %local_codes.3), channel_id=1, source_target_pairs={{0,16},{8,24},{16,0},{24,8},{1,17},{9,25},{17,1},{25,9},{2,18},{10... | collective-permute-start | bytes 417800 | tf_op jit(solution)/shard_map/ppermute | solution.py:20
  70.6 10.5 %collective-permute-start.18 = (f32[136,256]{1,0:T(8,128)S(1)}, f32[136,256]{1,0:T(8,128)S(1)}, u32[]{:S(2)}, u32[]{:S(2)}) collective-permute-start(f32[136,256]{1,0:T(8,128)S(1)} %local_codes.3), channel_id=1, source_target_pairs={{0,24},{8,16},{16,8},{24,0},{1,25},{9,17},{17,9},{25,1},{2,26},{10... | collective-permute-start | bytes 417800 | tf_op jit(solution)/shard_map/ppermute | solution.py:20
  72.0 9.0 %collective-permute-start.16 = (f32[136,256]{1,0:T(8,128)S(1)}, f32[136,256]{1,0:T(8,128)S(1)}, u32[]{:S(2)}, u32[]{:S(2)}) collective-permute-start(f32[136,256]{1,0:T(8,128)S(1)} %local_codes.3), channel_id=1, source_target_pairs={{0,8},{8,0},{16,24},{24,16},{1,9},{9,1},{17,25},{25,17},{2,10},{10... | collective-permute-start | bytes 417800 | tf_op jit(solution)/shard_map/ppermute | solution.py:20
  72.6 13.8 %collective-permute-start.6 = (s16[128,1152]{1,0:T(8,128)(2,1)S(1)}, s16[128,1152]{1,0:T(8,128)(2,1)S(1)}, u32[]{:S(2)}, u32[]{:S(2)}) collective-permute-start(s16[128,1152]{1,0:T(8,128)(2,1)S(1)} %update_part.1.refs_0_.refs_9_), channel_id=1, source_target_pairs={{0,8},{8,0},{16,24},{24,16},{1,9},{9,1},{17,25},{25,17},{2,10},{10... | collective-permute-start | bytes 884744 | tf_op jit(solution)/shard_map/ppermute | solution.py:20
  74.1 12.3 %collective-permute-start.7 = (s16[128,1152]{1,0:T(8,128)(2,1)S(1)}, s16[128,1152]{1,0:T(8,128)(2,1)S(1)}, u32[]{:S(2)}, u32[]{:S(2)}) collective-permute-start(s16[128,1152]{1,0:T(8,128)(2,1)S(1)} %update_part.1.refs_0_.refs_9_), channel_id=1, source_target_pairs={{0,16},{8,24},{16,0},{24,8},{1,17},{9,25},{17,1},{25,9},{2,18},{10... | collective-permute-start | bytes 884744 | tf_op jit(solution)/shard_map/ppermute | solution.py:20
  78.5 14.1 %collective-permute-start.8 = (s16[128,1152]{1,0:T(8,128)(2,1)S(1)}, s16[128,1152]{1,0:T(8,128)(2,1)S(1)}, u32[]{:S(2)}, u32[]{:S(2)}) collective-permute-start(s16[128,1152]{1,0:T(8,128)(2,1)S(1)} %update_part.1.refs_0_.refs_9_), channel_id=1, source_target_pairs={{0,24},{8,16},{16,8},{24,0},{1,25},{9,17},{17,9},{25,1},{2,26},{10... | collective-permute-start | bytes 884744 | tf_op jit(solution)/shard_map/ppermute | solution.py:20
